TPU v7x, 768 devices: a whole 4x8x12 slice. The times are simulated.
768 devices in a mesh: dp: 48 (over y_lo, z, core), section: 16 (over y_hi, x).
Axes of the slice: x: 4, y: 8 (y_hi: 4, y_lo: 2; y = y_hi * 2 + y_lo), z: 12, core: 2. Of those that a mesh axis runs over, the one named last changes fastest.
Arguments:
- hidden_act: bfloat16 [6144, 14336], P('dp', 'section'), may hold values from -6 to 6
- out_grad: bfloat16 [6144, 4608], P('dp'), may hold values from -0.076171875 to 0.076171875
- grad_accum: float32 [14336, 4608], P('section', 'dp'), may hold values from -6 to 6
- master_weight: float32 [14336, 4608], P('section', 'dp'), may hold values from -0.046875 to 0.046875
- adam_first: float32 [14336, 4608], P('section', 'dp'), may hold values from -2 to 2
- adam_second: float32 [14336, 4608], P('section', 'dp'), may hold values from 0.1 to 10
- decode_in: bfloat16 [4, 768, 14336], P(None, 'dp', 'section'), may hold values from -6 to 6
- residual_in: bfloat16 [4, 768, 4608], P(None, 'dp'), may hold values from -6 to 6
- norm_gain: bfloat16 [4608], P('section'), may hold values from 0.25 to 1.75
Outputs:
- weight_new: float32 [14336, 4608], P('section', 'dp')
- first_new: float32 [14336, 4608], P('section', 'dp')
- second_new: float32 [14336, 4608], P('section', 'dp')
- decoded: bfloat16 [4, 768, 4608], P(None, 'dp', 'section')
All inputs are finite; a program needn't handle non-finite values.
Results may differ from a plain program's by a relative error of at most 0.0039.
Values may be sent and summed in bfloat16 or wider, within the bound.
A program may use at most 64 MiB of HBM per device.

v0:
```python
import jax
import jax.numpy as jnp
from jax import lax
from jax.sharding import Mesh
from jax.sharding import PartitionSpec as P

DP = ("dp_0", "dp_1", "dp_2")


beta_first = 0.9
beta_second = 0.95
learn_rate = 0.002
decay_rate = 0.1
adam_eps = 1e-08
norm_eps = 1e-05
bias_first = 1.0 - 0.9**10
bias_second = 1.0 - 0.95**10


def reduced_to_own(tiles, axes, sequence):
    dims = [lax.axis_size(a) for a in axes]
    tiles = tiles.reshape(*dims, *tiles.shape[1:])
    tiles = tiles.transpose(*sequence, *range(len(axes), tiles.ndim))
    tiles = tiles.reshape(-1, *tiles.shape[len(axes) :])
    for k in sequence:
        tiles = lax.psum_scatter(tiles, axes[k], scatter_dimension=0, tiled=True)
    return tiles[0]


def in_blocks(array, dim, count):
    dims = array.shape
    tiles = array.reshape(*dims[:dim], count, dims[dim] // count, *dims[dim + 1 :])
    return jnp.moveaxis(tiles, dim, 0)


def scatter_axes(array, axes, sequence, dim):
    count = lax.axis_size(axes)
    return reduced_to_own(in_blocks(array, dim, count), axes, sequence)


def sum_at_owner(array, axis, dim):
    tiles = in_blocks(array, dim, lax.axis_size(axis))
    arrived = lax.all_to_all(tiles, axis, split_axis=0, concat_axis=0, tiled=True)
    return arrived.sum(axis=0)


def from_everyone(array, axis):
    count = lax.axis_size(axis)
    return lax.all_to_all(
        jnp.broadcast_to(array[None], (count, *array.shape)), axis, 0, 0, tiled=True
    )


def of_everyone(array, axis):
    return from_everyone(array, axis).sum(axis=0)


def per_device(
    hidden_act,
    out_grad,
    grad_accum,
    master_weight,
    adam_first,
    adam_second,
    decode_in,
    residual_in,
    norm_gain,
):
    contract_tokens = (((0,), (0,)), ((), ()))
    grad_term = lax.dot_general(
        out_grad, hidden_act, contract_tokens, preferred_element_type=jnp.float32
    )
    grad_share = scatter_axes(grad_term, DP, (2, 1, 0), 0)
    gradient = grad_share.T + grad_accum
    first_new = beta_first * adam_first + (1.0 - beta_first) * gradient
    second_new = beta_second * adam_second + (1.0 - beta_second) * gradient * gradient
    update = first_new / bias_first / (jnp.sqrt(second_new / bias_second) + adam_eps)
    weight_new = master_weight - learn_rate * (update + decay_rate * master_weight)
    weight_rounded = weight_new.astype(jnp.bfloat16)
    steps_count, roll_rows, hidden_local = decode_in.shape
    flat_in = decode_in.reshape(steps_count * roll_rows, hidden_local)
    partial_out = jnp.dot(
        flat_in,
        lax.all_gather(weight_rounded, DP, axis=1, tiled=True),
        preferred_element_type=jnp.float32,
    )
    width_all = partial_out.shape[1]
    share_width = width_all // lax.axis_size("section")
    resid_flat = residual_in.reshape(steps_count * roll_rows, width_all).astype(jnp.float32)
    offset = lax.axis_index("section") * share_width
    share_sum = sum_at_owner(partial_out, "section", 1)
    own_stream = lax.dynamic_slice_in_dim(resid_flat, offset, share_width, 1) + share_sum
    square_sum = of_everyone(jnp.sum(own_stream * own_stream, axis=1, keepdims=True), "section")
    mean_square = square_sum / width_all
    normed = own_stream * lax.rsqrt(mean_square + norm_eps) * norm_gain.astype(jnp.float32)
    decoded = normed.astype(jnp.bfloat16).reshape(steps_count, roll_rows, share_width)
    return (weight_new, first_new, second_new, decoded)


def solution(mesh):
    finer = Mesh(
        mesh.devices.reshape(2, 12, 2, mesh.shape["section"]), ("dp_0", "dp_1", "dp_2", "section")
    )
    in_specs = (
        P(DP, "section"),
        P(DP, None),
        P("section", DP),
        P("section", DP),
        P("section", DP),
        P("section", DP),
        P(None, DP, "section"),
        P(None, DP, None),
        P("section"),
    )
    out_specs = (P("section", DP), P("section", DP), P("section", DP), P(None, DP, "section"))
    return jax.shard_map(
        per_device, mesh=finer, in_specs=in_specs, out_specs=out_specs, check_vma=False
    )
```

profile of v0, /device:TPU:6, one launch (start us, length us, event | category | flops | bytes accessed | tf_op | source)
XLA Modules:
  0.0 386.2 jit_solution(5915897617707730296)
XLA Ops:
  7.2 0.0 copy-start
  7.2 0.0 reduce-scatter.4.cloned.1.call-start
  7.2 1.2 copy-done
  8.4 3.3 fusion.3
  11.7 6.0 %copy.14 = f32[2,12,2,96,896]{4,3,2,1,0:T(8,128)} copy(f32[2,12,2,96,896]{4,3,0,1,2:T(8,128)S(1)} %bitcast.27) | data formatting | bytes 33030144 | tf_op jit(solution)/shard_map/transpose | solution.py:23
  17.7 0.0 reduce-scatter.4.cloned.1.call-update
  17.7 0.0 reduce-scatter.6.cloned.1.call-start
  17.8 42.7 %reduce-scatter.4.cloned.1.call-done = f32[24,96,896]{2,1,0:T(8,128)} async-done(((f32[48,96,896]{2,1,0:T(8,128)}), f32[24,96,896]{2,1,0:T(8,128)}) %reduce-scatter.4.cloned.1.call-update) | async-done | bytes 8257552 | tf_op jit(solution)/shard_map/reduce_scatter | solution.py:26
  60.5 0.0 copy-start.1
  60.5 0.0 copy-start.2
  60.5 0.0 copy-start.3
  60.5 0.0 copy-start.4
  60.5 0.0 reduce-scatter.6.cloned.1.call-update
  60.5 0.0 reduce-scatter.8.cloned.1.call-start
  60.5 108.6 %reduce-scatter.6.cloned.1.call-done = f32[2,96,896]{2,1,0:T(8,128)} async-done(((f32[24,96,896]{2,1,0:T(8,128)}), f32[2,96,896]{2,1,0:T(8,128)}) %reduce-scatter.6.cloned.1.call-update) | async-done | bytes 688144 | tf_op jit(solution)/shard_map/reduce_scatter | solution.py:26
  169.1 0.0 reduce-scatter.8.cloned.1.call-update
  169.1 0.0 copy-start.5
  169.1 0.0 all-gather.2.cloned.1.call-start
  169.2 28.1 %reduce-scatter.8.cloned.1.call-done = f32[1,96,896]{2,1,0:T(8,128)} async-done(((f32[2,96,896]{2,1,0:T(8,128)}), f32[1,96,896]{2,1,0:T(8,128)}) %reduce-scatter.8.cloned.1.call-update) | async-done | bytes 344080 | tf_op jit(solution)/shard_map/reduce_scatter | solution.py:26
  197.3 0.0 copy-done.1
  197.3 0.0 copy-done.2
  197.3 0.0 copy-done.3
  197.3 0.0 copy-done.4
  197.3 2.2 fusion.1
  199.5 0.0 all-gather.2.cloned.1.call-update
  199.5 104.5 %all-gather.2.cloned.1.call-done = bf16[896,4608]{0,1:T(8,128)(2,1)} async-done(((bf16[896,96]{0,1:T(8,128)(2,1)}), bf16[896,4608]{0,1:T(8,128)(2,1)}) %all-gather.2.cloned.1.call-update) | async-done | bytes 8257552 | tf_op jit(solution)/shard_map/all_gather | solution.py:84
  304.1 0.0 copy-done.5
  304.1 6.0 %convolution_bitcast_fusion = f32[64,4608]{1,0:T(8,128)S(1)} fusion(bf16[896,4608]{0,1:T(8,128)(2,1)} %all-gather.2.cloned.1.call-done, bf16[64,896]{1,0:T(8,128)(2,1)S(1)} %bitcast.30), kind=kOutput, calls=%fused_computation | convolution fusion | flops 528482304 | bytes 9551872 | tf_op jit(solution)/shard_map/dot_general | solution.py:82
  310.0 2.1 reshape.38
  312.2 3.1 copy.17
  315.2 8.8 %all-to-all-start = ((f32[16,64,288]{2,1,0:T(8,128)}), f32[16,64,288]{2,1,0:T(8,128)S(1)}, u32[]{:S(2)}, u32[]{:S(2)}) async-start(f32[16,64,288]{2,1,0:T(8,128)} %bitcast.29), calls=%async_computation.3 | async-start | bytes 3145728 | tf_op jit(solution)/shard_map/all_to_all | solution.py:43
  324.0 0.0 copy-start.6
  324.1 36.3 %all-to-all-done = f32[16,64,288]{2,1,0:T(8,128)S(1)} async-done(((f32[16,64,288]{2,1,0:T(8,128)}), f32[16,64,288]{2,1,0:T(8,128)S(1)}, u32[]{:S(2)}, u32[]{:S(2)}) %all-to-all-start) | async-done | bytes 1179680 | tf_op jit(solution)/shard_map/all_to_all | solution.py:43
  360.4 0.1 reduce_sum.27
  360.5 1.0 multiply_reduce_fusion
  361.5 0.6 broadcast_in_dim.2
  362.2 7.9 %all-to-all-start.1 = ((f32[16,64,1]{1,2,0:T(1,128)}), f32[16,64,1]{1,2,0:T(1,128)S(1)}, u32[]{:S(2)}, u32[]{:S(2)}) async-start(f32[16,64,1]{1,2,0:T(1,128)} %broadcast_in_dim.2), calls=%async_computation.4 | async-start | bytes 16384 | tf_op jit(solution)/shard_map/all_to_all | solution.py:49
  370.1 0.0 copy-done.6
  370.1 7.9 %all-to-all-done.1 = f32[16,64,1]{1,2,0:T(1,128)S(1)} async-done(((f32[16,64,1]{1,2,0:T(1,128)}), f32[16,64,1]{1,2,0:T(1,128)S(1)}, u32[]{:S(2)}, u32[]{:S(2)}) %all-to-all-start.1) | async-done | bytes 4128 | tf_op jit(solution)/shard_map/all_to_all | solution.py:49
  378.1 1.6 multiply_convert_fusion
  (3 shorter events, 0.0 us)
Async XLA Ops:
  7.2 1.3 copy-start
  7.2 53.3 %reduce-scatter.4.cloned.1.call-start = ((), (), s32[]{:S(2)}) async-start(), calls=%async_computation.5 | async-start | bytes 24772608 | tf_op jit(solution)/shard_map/reduce_scatter | solution.py:26
  17.7 151.4 %reduce-scatter.6.cloned.1.call-start = ((), (), s32[]{:S(2)}) async-start(), calls=%async_computation.6 | async-start | bytes 8945664 | tf_op jit(solution)/shard_map/reduce_scatter | solution.py:26
  60.5 136.8 %copy-start.1 = (f32[896,96]{0,1:T(8,128)S(1)}, f32[896,96]{0,1:T(8,128)}, u32[]{:S(2)}) copy-start(f32[896,96]{0,1:T(8,128)} %param.12) | copy-start | bytes 1032196
  60.5 136.8 %copy-start.2 = (f32[896,96]{0,1:T(8,128)S(1)}, f32[896,96]{0,1:T(8,128)}, u32[]{:S(2)}) copy-start(f32[896,96]{0,1:T(8,128)} %param.11) | copy-start | bytes 1032196
  60.5 136.8 %copy-start.3 = (f32[896,96]{0,1:T(8,128)S(1)}, f32[896,96]{0,1:T(8,128)}, u32[]{:S(2)}) copy-start(f32[896,96]{0,1:T(8,128)} %param.13) | copy-start | bytes 1032196
  60.5 136.8 %copy-start.4 = (f32[896,96]{0,1:T(8,128)S(1)}, f32[896,96]{0,1:T(8,128)}, u32[]{:S(2)}) copy-start(f32[896,96]{0,1:T(8,128)} %param.14) | copy-start | bytes 1032196
  60.5 136.8 %reduce-scatter.8.cloned.1.call-start = ((), (), s32[]{:S(2)}) async-start(), calls=%async_computation.7 | async-start | bytes 1032192 | tf_op jit(solution)/shard_map/reduce_scatter | solution.py:26
  169.1 134.9 %copy-start.5 = (bf16[4,16,896]{2,1,0:T(8,128)(2,1)S(1)}, bf16[4,16,896]{2,1,0:T(8,128)(2,1)}, u32[]{:S(2)}) copy-start(bf16[4,16,896]{2,1,0:T(8,128)(2,1)} %param.15) | copy-start | bytes 344068
  169.1 134.9 %all-gather.2.cloned.1.call-start = ((), (), s32[]{:S(2)}) async-start(), calls=%async_computation.8 | async-start | bytes 8429568 | tf_op jit(solution)/shard_map/all_gather | solution.py:84
  315.2 45.2 %all-to-all-start = ((f32[16,64,288]{2,1,0:T(8,128)}), f32[16,64,288]{2,1,0:T(8,128)S(1)}, u32[]{:S(2)}, u32[]{:S(2)}) async-start(f32[16,64,288]{2,1,0:T(8,128)} %bitcast.29), calls=%async_computation.3 | async-start | bytes 3145728 | tf_op jit(solution)/shard_map/all_to_all | solution.py:43
  324.0 46.1 %copy-start.6 = (bf16[288]{0:T(512)(128)(2,1)S(1)}, bf16[288]{0:T(512)(128)(2,1)}, u32[]{:S(2)}) copy-start(bf16[288]{0:T(512)(128)(2,1)} %param.17) | copy-start | bytes 1732
  362.2 15.9 %all-to-all-start.1 = ((f32[16,64,1]{1,2,0:T(1,128)}), f32[16,64,1]{1,2,0:T(1,128)S(1)}, u32[]{:S(2)}, u32[]{:S(2)}) async-start(f32[16,64,1]{1,2,0:T(1,128)} %broadcast_in_dim.2), calls=%async_computation.4 | async-start | bytes 16384 | tf_op jit(solution)/shard_map/all_to_all | solution.py:49
Sparse Core Ops, SparseCore 0:
  17.9 42.5 reduce-scatter.3
  63.6 105.4 reduce-scatter.5
  172.2 25.0 reduce-scatter.7
  199.6 104.3 all-gather.1
where the time goes:
time: 390 us; the launch traced here: 386 us
  waiting for transfers between devices  328 us (84%)
  starting transfers between devices  16.9 us (4%)
  between operations  13.8 us (4%)
  local copies, waits for them, and re-layouts  13 us (3%)
  matrix products  9.24 us (2%)
  other arithmetic  4.93 us (1%)
    reduce_scatter x3, waiting for transfers between devices, reduced_to_own(): tiles = lax.psum_scatter(tiles, axes[k], scatter_dimension=0, tiled=True)  179 us
    all_gather x1, waiting for transfers between devices, per_device(): lax.all_gather(weight_rounded, DP, axis=1, tiled=True)  105 us
    all_to_all x1, waiting for transfers between devices, sum_at_owner(): lax.all_to_all(tiles, axis, split_axis=0, concat_axis=0, tiled=True)  36.3 us
    all_to_all x1, starting transfers between devices, sum_at_owner(): lax.all_to_all(tiles, axis, split_axis=0, concat_axis=0, tiled=True)  8.81 us
    all_to_all x1, starting transfers between devices, from_everyone(): lax.all_to_all(jnp.broadcast_to(array[None], (count, *array.shape)), axis...  7.95 us
    all_to_all x1, waiting for transfers between devices, from_everyone(): lax.all_to_all(jnp.broadcast_to(array[None], (count, *array.shape)), axis...  7.94 us
  transfers between devices with their start and end apart: 6, of which 6 were waited for; matrix products, arithmetic and copies ran while one was open for 0% of the time, Pallas kernels for 0%

commit v1 on v0

v1 whole, which is shorter than its diff:
```python
import functools

import jax
import jax.numpy as jnp
from jax import lax
from jax.experimental import pallas as pl
from jax.experimental.pallas import tpu as pltpu
from jax.sharding import Mesh
from jax.sharding import PartitionSpec as P

DP = ("yl", "z", "c")
SECTION = ("yh", "x")
MESH_ID = pl.DeviceIdType.MESH

beta_first = 0.9
beta_second = 0.95
learn_rate = 0.002
decay_rate = 0.1
adam_eps = 1e-08
norm_eps = 1e-05
bias_first = 1.0 - 0.9**10
bias_second = 1.0 - 0.95**10


def remote(src, dst, send_sem, recv_sem, target):
    return pltpu.make_async_remote_copy(
        src_ref=src,
        dst_ref=dst,
        send_sem=send_sem,
        recv_sem=recv_sem,
        device_id=target,
        device_id_type=MESH_ID,
    )


def greet(targets):
    barrier = pltpu.get_barrier_semaphore()
    for target in targets:
        pl.semaphore_signal(barrier, inc=1, device_id=target, device_id_type=MESH_ID)
    pl.semaphore_wait(barrier, len(targets))


def grad_kernel(
    nz,
    h_ref,
    ot_ref,
    g_ref,
    hall,
    oall,
    part,
    sbuf,
    rbuf,
    h_send,
    h_recv,
    o_send,
    o_recv,
    r_send,
    r_recv,
):
    yl, z, c = lax.axis_index("yl"), lax.axis_index("z"), lax.axis_index("c")
    steps = nz // 2
    tokens, hidden = h_ref.shape
    rows = ot_ref.shape[3]
    half = rows // 2
    cut = (hidden // 256) * 128 + 128 if hidden > 128 else hidden
    lanes = [(0, cut), (cut, hidden - cut)] if hidden > cut else [(0, hidden)]
    core = {"c": 1 - c}
    across = {"yl": 1 - yl}
    diagonal = {"yl": 1 - yl, "c": 1 - c}
    up = {"z": lax.rem(z + 1, nz)}
    down = {"z": lax.rem(z + nz - 1, nz)}
    greet([core, across, diagonal, up, down])

    def h_copy(slot, src, target, index):
        return remote(
            src, hall.at[pl.ds(slot * tokens, tokens)], h_send.at[index], h_recv.at[index], target
        )

    h_across = h_copy(2, h_ref, across, 1)
    h_core = h_copy(1, h_ref, core, 0)
    h_forward = h_copy(3, hall.at[pl.ds(2 * tokens, tokens)], core, 2)
    h_across.start()
    h_core.start()

    def block_at(q):
        far = steps - (q + 1) // 2
        return lax.rem(jnp.where(q % 2 == 1, z + far, z + nz - far), nz)

    peers = [(1, core, yl, 1 - c), (2, across, 1 - yl, c), (3, diagonal, 1 - yl, 1 - c)]

    def o_copy(q, slot, target, to_yl, to_c):
        return remote(
            ot_ref.at[to_yl, block_at(q), to_c],
            oall.at[q, :, pl.ds(slot * tokens, tokens)],
            o_send.at[slot - 1, q],
            o_recv.at[slot - 1, q],
            target,
        )

    def send_blocks(q, carry):
        for peer in peers:
            o_copy(q, *peer).start()
        oall[q, :, pl.ds(0, tokens)] = ot_ref[yl, block_at(q), c]
        return carry

    lax.fori_loop(0, nz, send_blocks, 0)
    hall[pl.ds(0, tokens), :] = h_ref[...]
    h_across.wait_recv()
    h_forward.start()
    h_core.wait_recv()
    h_forward.wait_recv()

    def compute(q, slot, way):
        for peer in peers:
            o_copy(q, *peer).wait_recv()
        part[slot, way] = jnp.dot(oall[q], hall[...], preferred_element_type=jnp.float32)

    def r_copy(way, sub, n, t):
        first, width = lanes[n]
        spot = (way, sub, t, slice(None), pl.ds(first, width))
        return remote(
            sbuf.at[spot],
            rbuf.at[spot],
            r_send.at[way, sub, n, t],
            r_recv.at[way, sub, n, t],
            (up, down)[way],
        )

    def push(way, sub, n, t, slot, src_way, receive):
        first, width = lanes[n]
        value = part[slot, src_way, pl.ds(sub * half, half), pl.ds(first, width)]
        if receive:
            r_copy(way, sub, n, t - 1).wait_recv()
            value += rbuf[way, sub, t - 1, :, pl.ds(first, width)].astype(jnp.float32)
        sbuf[way, sub, t, :, pl.ds(first, width)] = value.astype(jnp.bfloat16)
        r_copy(way, sub, n, t).start()

    compute(0, 0, 0)
    for n in range(len(lanes)):
        push(0, 0, n, 0, 0, 0, False)
        push(1, 1, n, 0, 0, 0, False)

    def fill(t):
        slot = lax.rem(t, 2)
        compute(2 * t - 1, slot, 0)
        compute(2 * t, slot, 1)

    fill(1)
    for sub in range(2):
        for n in range(len(lanes)):
            push(0, sub, n, 1, 1, 0, sub == 0)
            push(1, 1 - sub, n, 1, 1, 1, sub == 0)

    def step(t, carry):
        fill(t)
        slot = lax.rem(t, 2)
        for sub in range(2):
            for n in range(len(lanes)):
                push(0, sub, n, t, slot, 0, True)
                push(1, 1 - sub, n, t, slot, 1, True)
        return carry

    lax.fori_loop(2, steps, step, 0)
    compute(nz - 1, 0, 0)
    for sub in range(2):
        for n, (first, width) in enumerate(lanes):
            value = part[0, 0, pl.ds(sub * half, half), pl.ds(first, width)]
            for way in range(2):
                r_copy(way, sub, n, steps - 1).wait_recv()
                value += rbuf[way, sub, steps - 1, :, pl.ds(first, width)].astype(jnp.float32)
            g_ref[pl.ds(sub * half, half), pl.ds(first, width)] = value

    h_across.wait_send()
    h_core.wait_send()
    h_forward.wait_send()

    def drain_blocks(q, carry):
        for peer in peers:
            o_copy(q, *peer).wait_send()
        return carry

    lax.fori_loop(0, nz, drain_blocks, 0)
    for n in range(len(lanes)):
        r_copy(0, 0, n, 0).wait_send()
        r_copy(1, 1, n, 0).wait_send()

    def drain(t, carry):
        for way in range(2):
            for sub in range(2):
                for n in range(len(lanes)):
                    r_copy(way, sub, n, t).wait_send()
        return carry

    lax.fori_loop(1, steps, drain, 0)


def gradient_share(nz, hidden_act, out_t):
    tokens, hidden = hidden_act.shape
    rows = out_t.shape[3]
    steps = nz // 2
    vmem = pl.BlockSpec(memory_space=pltpu.VMEM)
    return pl.pallas_call(
        functools.partial(grad_kernel, nz),
        out_shape=jax.ShapeDtypeStruct((rows, hidden), jnp.float32),
        in_specs=[vmem, vmem],
        out_specs=vmem,
        scratch_shapes=[
            pltpu.VMEM((4 * tokens, hidden), jnp.bfloat16),
            pltpu.VMEM((nz, rows, 4 * tokens), jnp.bfloat16),
            pltpu.VMEM((2, 2, rows, hidden), jnp.float32),
            pltpu.VMEM((2, 2, steps, rows // 2, hidden), jnp.bfloat16),
            pltpu.VMEM((2, 2, steps, rows // 2, hidden), jnp.bfloat16),
            pltpu.SemaphoreType.DMA((3,)),
            pltpu.SemaphoreType.DMA((3,)),
            pltpu.SemaphoreType.DMA((3, nz)),
            pltpu.SemaphoreType.DMA((3, nz)),
            pltpu.SemaphoreType.DMA((2, 2, 2, steps)),
            pltpu.SemaphoreType.DMA((2, 2, 2, steps)),
        ],
        compiler_params=pltpu.CompilerParams(collective_id=0, has_side_effects=True),
        cost_estimate=pl.CostEstimate(
            flops=2 * nz * rows * hidden * 4 * tokens, bytes_accessed=3000000, transcendentals=0
        ),
        name="gradient",
    )(hidden_act, out_t)


def decode_kernel(
    nz,
    w_ref,
    x_ref,
    resid_ref,
    gain_ref,
    out_ref,
    xb,
    wall,
    pbuf,
    xbuf,
    ysend,
    ybuf,
    ss_out,
    ss_in,
    p_send,
    p_recv,
    w_send,
    w_recv,
    c_send,
    c_recv,
    own_send,
    own_recv,
    x_send,
    x_recv,
    y_send,
    y_recv,
    s_send,
    s_recv,
):
    yl, z, c = lax.axis_index("yl"), lax.axis_index("z"), lax.axis_index("c")
    yh, x = lax.axis_index("yh"), lax.axis_index("x")
    steps = nz // 2
    cols, hidden = w_ref.shape
    half = cols // 2
    roll = x_ref.shape[0]
    per = 2 * nz // 8
    core = {"c": 1 - c}
    across = {"yl": 1 - yl}
    ring = ({"z": lax.rem(z + 1, nz)}, {"z": lax.rem(z + nz - 1, nz)})
    place = yh * 4 + x
    section = []
    for r in range(1, 16):
        other = lax.rem(place + r, 16)
        section.append({"yh": other // 4, "x": lax.rem(other, 4)})
    flipped = [{"yl": 1 - yl, "yh": other} for other in range(4)]
    greet([core, *ring, *section, *flipped])

    pair = remote(x_ref, xb.at[pl.ds(yl * roll, roll)], p_send.at[0], p_recv.at[0], across)
    own = remote(w_ref, wall.at[z, c], own_send.at[0], own_recv.at[0], core)

    def w_copy(way, sub, t, first=False):
        block = lax.rem(z + nz - t, nz) if way == 0 else lax.rem(z + t, nz)
        spot = wall.at[block, c, pl.ds(sub * half, half)]
        return remote(
            w_ref.at[pl.ds(sub * half, half)] if first else spot,
            spot,
            w_send.at[way, sub, t],
            w_recv.at[way, sub, t],
            ring[way],
        )

    def c_copy(way, sub, t):
        block = lax.rem(z + 2 * nz - 1 - t, nz) if way == 0 else lax.rem(z + 1 + t, nz)
        spot = wall.at[block, c, pl.ds(sub * half, half)]
        return remote(spot, spot, c_send.at[way, sub, t], c_recv.at[way, sub, t], core)

    for sub in range(2):
        for way in range(2):
            w_copy(way, sub, 0, True).start()
    own.start()
    pair.start()
    wall[z, c] = w_ref[...]
    xb[pl.ds(yl * roll, roll), :] = x_ref[...]
    pair.wait_recv()
    own.wait_recv()

    def x_copy(rel, j, k):
        return remote(
            pbuf.at[j, k],
            xbuf.at[rel - 1, j // 4, k],
            x_send.at[rel - 1, j // 4, k],
            x_recv.at[rel - 1, j // 4, k],
            {"x": lax.rem(x + rel, 4)},
        )

    def multiply(block):
        product = lax.dot_general(
            wall[block].reshape(2 * cols, hidden),
            xb[...],
            (((1,), (1,)), ((), ())),
            preferred_element_type=jnp.float32,
        )
        for lane in range(2):
            piece = 2 * block + lane
            j, k = piece // per, lax.rem(piece, per)
            pbuf[j, k] = product[lane * cols : (lane + 1) * cols].astype(jnp.bfloat16)
            rel = lax.rem(lax.rem(j, 4) + 4 - x, 4)

            @pl.when(rel != 0)
            def _():
                x_copy(rel, j, k).start()

    multiply(z)

    def pass_on(way, sub, t, last):
        w_copy(way, sub, t).wait_recv()
        if not last:
            w_copy(way, sub, t + 1).start()
        c_copy(way, sub, t).start()

    def step(t, carry):
        for way in range(2):
            pass_on(way, way, t, False)
        for way in range(2):
            w_copy(way, 1 - way, t).wait_recv()

            @pl.when(t < steps - 2)
            def _(way=way):
                w_copy(way, 1 - way, t + 1).start()

            c_copy(way, 1 - way, t).start()
        for way in range(2):
            for sub in range(2):
                c_copy(way, sub, t).wait_recv()
        multiply(lax.rem(z + nz - 1 - t, nz))
        multiply(lax.rem(z + 1 + t, nz))
        return carry

    lax.fori_loop(0, steps - 1, step, 0)
    for way in range(2):
        pass_on(way, way, steps - 1, True)
    for way in range(2):
        c_copy(way, way, steps - 1).wait_recv()
    multiply(lax.rem(z + steps, nz))

    def y_copy(to_yl, jj):
        return remote(
            ysend.at[to_yl, jj],
            ybuf.at[yh],
            y_send.at[to_yl, jj],
            y_recv.at[yh],
            {"yl": to_yl, "yh": 2 * yl + jj},
        )

    share = per * cols
    for jj in range(2):
        total = pbuf[jj * 4 + x].astype(jnp.float32)
        for rel in range(1, 4):
            for k in range(per):
                x_copy(rel, jj * 4, k).wait_recv()
            total += xbuf[rel - 1, jj].astype(jnp.float32)
        total = total.reshape(share, 2 * roll)
        for to_yl in range(2):
            rows = slice(to_yl * roll, (to_yl + 1) * roll)
            packed = jnp.concatenate(
                [total[: share // 2, rows], total[share // 2 :, rows]], axis=1
            ).astype(jnp.bfloat16)
            mine = jnp.logical_and(yl == to_yl, yh == 2 * yl + jj)

            @pl.when(mine)
            def _(packed=packed):
                ybuf[yh] = packed

            @pl.when(jnp.logical_not(mine))
            def _(packed=packed, to_yl=to_yl, jj=jj):
                ysend[to_yl, jj] = packed
                y_copy(to_yl, jj).start()

    stream = resid_ref[...]
    for source in range(4):
        mine = jnp.logical_and(yh == source, yh // 2 == yl)

        @pl.when(jnp.logical_not(mine))
        def _(source=source):
            remote(
                ysend.at[0, 0], ybuf.at[source], y_send.at[0, 0], y_recv.at[source], across
            ).wait_recv()

        stream += ybuf[source].astype(jnp.float32)

    square = jnp.sum(stream * stream, axis=0, keepdims=True)
    square = jnp.broadcast_to(square, (8, 2 * roll))
    square = square + pltpu.roll(square, roll, 1)
    ss_out[...] = square

    def s_copy(r):
        return remote(ss_out, ss_in.at[r - 1], s_send.at[r - 1], s_recv.at[r - 1], section[r - 1])

    for r in range(1, 16):
        s_copy(r).start()
    for r in range(1, 16):
        s_copy(r).wait_recv()
        square += ss_in[r - 1]
    scale = lax.rsqrt(square * (1.0 / (16 * share)) + norm_eps)
    out_ref[...] = (stream * scale[0:1] * gain_ref[...]).astype(jnp.bfloat16)

    pair.wait_send()
    own.wait_send()

    def drain(t, carry):
        for way in range(2):
            for sub in range(2):
                w_copy(way, sub, t).wait_send()
                c_copy(way, sub, t).wait_send()
        return carry

    lax.fori_loop(0, steps - 1, drain, 0)
    for way in range(2):
        w_copy(way, way, steps - 1).wait_send()
        c_copy(way, way, steps - 1).wait_send()
    for rel in range(1, 4):
        for jj in range(2):
            for k in range(per):
                x_copy(rel, jj * 4, k).wait_send()
    for jj in range(2):
        for to_yl in range(2):
            mine = jnp.logical_and(yl == to_yl, yh == 2 * yl + jj)

            @pl.when(jnp.logical_not(mine))
            def _(to_yl=to_yl, jj=jj):
                y_copy(to_yl, jj).wait_send()

    for r in range(1, 16):
        s_copy(r).wait_send()


def decode(nz, w, x, resid, gain):
    cols, hidden = w.shape
    roll = x.shape[0]
    steps = nz // 2
    per = 2 * nz // 8
    vmem = pl.BlockSpec(memory_space=pltpu.VMEM)
    dma = pltpu.SemaphoreType.DMA
    return pl.pallas_call(
        functools.partial(decode_kernel, nz),
        out_shape=jax.ShapeDtypeStruct(resid.shape, jnp.bfloat16),
        in_specs=[vmem] * 4,
        out_specs=vmem,
        scratch_shapes=[
            pltpu.VMEM((2 * roll, hidden), jnp.bfloat16),
            pltpu.VMEM((nz, 2, cols, hidden), jnp.bfloat16),
            pltpu.VMEM((8, per, cols, 2 * roll), jnp.bfloat16),
            pltpu.VMEM((3, 2, per, cols, 2 * roll), jnp.bfloat16),
            pltpu.VMEM((2, 2, *resid.shape), jnp.bfloat16),
            pltpu.VMEM((4, *resid.shape), jnp.bfloat16),
            pltpu.VMEM((8, 2 * roll), jnp.float32),
            pltpu.VMEM((15, 8, 2 * roll), jnp.float32),
            dma((1,)),
            dma((1,)),
            dma((2, 2, steps)),
            dma((2, 2, steps)),
            dma((2, 2, steps)),
            dma((2, 2, steps)),
            dma((1,)),
            dma((1,)),
            dma((3, 2, per)),
            dma((3, 2, per)),
            dma((2, 2)),
            dma((4,)),
            dma((15,)),
            dma((15,)),
        ],
        compiler_params=pltpu.CompilerParams(collective_id=1, has_side_effects=True),
        cost_estimate=pl.CostEstimate(
            flops=8 * nz * cols * hidden * roll, bytes_accessed=1000000, transcendentals=0
        ),
        name="decode",
    )(w, x, resid, gain)


def per_device(
    hidden_act,
    out_grad,
    grad_accum,
    master_weight,
    adam_first,
    adam_second,
    decode_in,
    residual_in,
    norm_gain,
):
    nz = lax.axis_size("z")
    tokens = hidden_act.shape[0]
    rows = master_weight.shape[1]
    out_t = out_grad.T.reshape(2, nz, 2, rows, tokens)
    grad_share = gradient_share(nz, hidden_act, out_t)
    gradient = grad_share.T + grad_accum
    first_new = beta_first * adam_first + (1.0 - beta_first) * gradient
    second_new = beta_second * adam_second + (1.0 - beta_second) * gradient * gradient
    update = first_new / bias_first / (jnp.sqrt(second_new / bias_second) + adam_eps)
    weight_new = master_weight - learn_rate * (update + decay_rate * master_weight)
    weight_rounded = weight_new.astype(jnp.bfloat16)
    steps_count, roll_rows, hidden_local = decode_in.shape
    flat_rows = steps_count * roll_rows
    flat_in = decode_in.reshape(flat_rows, hidden_local)
    share_width = norm_gain.shape[0]
    middle = share_width // 2
    resid_flat = residual_in.reshape(flat_rows, -1)
    offset = lax.axis_index(SECTION) * share_width
    resid = lax.dynamic_slice_in_dim(resid_flat, offset, share_width, 1)
    resid = resid.astype(jnp.float32).T
    resid = jnp.concatenate([resid[:middle], resid[middle:]], axis=1)
    gain = norm_gain.astype(jnp.float32).reshape(2, middle, 1)
    gain = jnp.broadcast_to(gain, (2, middle, flat_rows))
    gain = jnp.concatenate([gain[0], gain[1]], axis=1)
    packed = decode(nz, weight_rounded.T, flat_in, resid, gain)
    decoded = jnp.concatenate([packed[:, :flat_rows], packed[:, flat_rows:]], axis=0).T
    decoded = decoded.reshape(steps_count, roll_rows, share_width)
    return (weight_new, first_new, second_new, decoded)


def solution(mesh):
    finer = Mesh(mesh.devices.reshape(2, 12, 2, 4, 4), ("yl", "z", "c", "yh", "x"))
    in_specs = (
        P(DP, SECTION),
        P(DP, None),
        P(SECTION, DP),
        P(SECTION, DP),
        P(SECTION, DP),
        P(SECTION, DP),
        P(None, DP, SECTION),
        P(None, DP, None),
        P(SECTION),
    )
    out_specs = (P(SECTION, DP), P(SECTION, DP), P(SECTION, DP), P(None, DP, SECTION))
    return jax.shard_map(
        per_device, mesh=finer, in_specs=in_specs, out_specs=out_specs, check_vma=False
    )
```

time: 390 us -> 112 us (0.29)
  waiting for transfers between devices: 328 us -> 0 us
  Pallas kernels: 0 us -> 103 us
  starting transfers between devices: 16.9 us -> 0 us
  between operations: 13.8 us -> 0.75 us
  matrix products: 9.24 us -> 0 us
  local copies, waits for them, and re-layouts: 13 us -> 4.56 us
    reduce_scatter x3 -> x0, waiting for transfers between devices: 179 us -> none  [reduced_to_own(): tiles = lax.psum_scatter(tiles, axes[k], scatter_dimension=0, tiled=True)]
    all_gather x1 -> x0, waiting for transfers between devices: 105 us -> none  [per_device(): lax.all_gather(weight_rounded, DP, axis=1, tiled=True)]
    pallas_call x0 -> x2, Pallas kernels: none -> 103 us  [the longest x1 52.3 us: decode(): pl.pallas_call(functools.partial(decode_kernel, nz), out_shape=jax.ShapeD...]
    all_to_all x2 -> x0, waiting for transfers between devices: 44.3 us -> none  [the longest x1 36.3 us: sum_at_owner(): lax.all_to_all(tiles, axis, split_axis=0, concat_axis=0, tiled=True)]
    all_to_all x2 -> x0, starting transfers between devices: 16.8 us -> none  [the longest x1 8.81 us: sum_at_owner(): lax.all_to_all(tiles, axis, split_axis=0, concat_axis=0, tiled=True)]
    dot_general x2 -> x0, matrix products: 9.24 us -> none  [the longest x1 5.96 us: per_device(): jnp.dot(flat_in, lax.all_gather(weight_rounded, DP, axis=1, tiled=True),...]
    reshape x2 -> x0, local copies, waits for them, and re-layouts: 5.19 us -> none  [in_blocks(): array.reshape(*dims[:dim], count, dims[dim] // count, *dims[dim + 1:])]
  transfers between devices with their start and end apart: 6 -> 0, of which waited for: 6 -> 0; matrix products, arithmetic and copies ran while one was open for 0% -> 0% of each run, Pallas kernels for 0% -> 0%
where the time goes in v1:
time: 112 us; the launch traced here: 111 us
  Pallas kernels  103 us (92%)
  local copies, waits for them, and re-layouts  4.56 us (4%)
  other arithmetic  2.99 us (3%)
    pallas_call x1, Pallas kernels, decode(): pl.pallas_call(functools.partial(decode_kernel, nz), out_shape=jax.ShapeD...  52.3 us
    pallas_call x1, Pallas kernels, gradient_share(): pl.pallas_call(functools.partial(grad_kernel, nz), out_shape=jax.ShapeDty...  50.7 us
    transpose x1, local copies, waits for them, and re-layouts, per_device(): out_t = out_grad.T.reshape(2, nz, 2, rows, tokens)  2.44 us

profile of v1, /device:TPU:6, one launch (start us, length us, event | category | flops | bytes accessed | tf_op | source)
XLA Modules:
  0.0 111.4 jit_solution(11033355732967425809)
XLA Ops:
  0.6 0.0 copy-start
  0.6 2.4 %copy.16 = bf16[4608,128]{1,0:T(8,128)(2,1)} copy(bf16[4608,128]{0,1:T(8,128)(2,1)} %bitcast.20) | data formatting | bytes 2359296 | tf_op jit(solution)/shard_map/transpose | solution.py:513
  3.1 0.0 copy-start.1
  3.1 0.0 copy-start.2
  3.1 0.0 copy-start.3
  3.1 0.0 copy-start.4
  3.1 50.7 %gradient.1 = f32[96,896]{1,0:T(8,128)} custom-call(bf16[128,896]{1,0:T(8,128)(2,1)} %h_ref.1, bf16[2,12,2,96,128]{4,3,2,1,0:T(8,128)(2,1)} %bitcast.21), custom_call_target="tpu_custom_call" | custom-call | flops 1056964608 | bytes 3000000 | tf_op jit(solution)/shard_map/gradient/pallas_call | solution.py:202
  53.8 0.0 copy-done.1
  53.8 0.0 copy-done.2
  53.9 0.0 copy-done.3
  53.9 0.0 copy-done.4
  53.9 0.0 copy-start.5
  53.9 2.2 %convert_bitcast_fusion = (bf16[96,896]{1,0:T(8,128)(2,1)}, f32[896,96]{0,1:T(8,128)}, f32[896,96]{0,1:T(8,128)}, f32[896,96]{0,1:T(8,128)}) fusion(f32[896,96]{0,1:T(8,128)S(1)} %copy-done.1, f32[896,96]{0,1:T(8,128)S(1)} %copy-done.2, f32[96,896]{1,0:T(8,128)} %gradient.1, f32[896,96]{0,1:T(8,128)S(1)} %copy-done.3, f32[896,96]{0,1:T(8,128)S(1)} %copy-done.4), kind=kLoop, calls=%fused_computation.5 | loop fusion | flops 1462272 | bytes 2924544 | tf_op jit(solution)/shard_map/transpose | solution.py:534
  56.1 0.0 copy-done
  56.1 0.1 constant_dynamic-slice_fusion
  56.2 0.1 copy.19
  56.3 0.0 copy-done.5
  56.3 0.1 fusion.4
  56.4 0.1 broadcast_in_dim.8
  56.5 0.1 broadcast_in_dim.7
  56.6 0.8 pad_maximum_fusion
  57.4 52.3 %decode.1 = bf16[144,128]{1,0:T(8,128)(2,1)} custom-call(bf16[96,896]{1,0:T(8,128)(2,1)} %get-tuple-element.8.w_ref, bf16[64,896]{1,0:T(8,128)(2,1)} %bitcast.23, f32[144,128]{1,0:T(8,128)} %get-tuple-element.18.resid_ref, f32[144,128]{1,0:T(8,128)} %get-tuple-element.19.gain_ref), custom_call_target="tpu_custom_call" | custom-call | flops 528482304 | bytes 1000000 | tf_op jit(solution)/shard_map/decode/pallas_call | solution.py:462
  109.7 0.9 fusion.3
  110.7 0.7 copy.18
  (3 shorter events, 0.0 us)
Async XLA Ops:
  0.6 55.4 %copy-start = (bf16[4,16,4608]{2,1,0:T(8,128)(2,1)S(1)}, bf16[4,16,4608]{2,1,0:T(8,128)(2,1)}, u32[]{:S(2)}) copy-start(bf16[4,16,4608]{2,1,0:T(8,128)(2,1)} %param.16) | copy-start | bytes 1769476
  3.1 50.8 %copy-start.1 = (f32[896,96]{0,1:T(8,128)S(1)}, f32[896,96]{0,1:T(8,128)}, u32[]{:S(2)}) copy-start(f32[896,96]{0,1:T(8,128)} %param.12) | copy-start | bytes 1032196
  3.1 50.8 %copy-start.2 = (f32[896,96]{0,1:T(8,128)S(1)}, f32[896,96]{0,1:T(8,128)}, u32[]{:S(2)}) copy-start(f32[896,96]{0,1:T(8,128)} %param.11) | copy-start | bytes 1032196
  3.1 50.8 %copy-start.3 = (f32[896,96]{0,1:T(8,128)S(1)}, f32[896,96]{0,1:T(8,128)}, u32[]{:S(2)}) copy-start(f32[896,96]{0,1:T(8,128)} %param.13) | copy-start | bytes 1032196
  3.1 50.8 %copy-start.4 = (f32[896,96]{0,1:T(8,128)S(1)}, f32[896,96]{0,1:T(8,128)}, u32[]{:S(2)}) copy-start(f32[896,96]{0,1:T(8,128)} %param.14) | copy-start | bytes 1032196
  53.9 2.4 %copy-start.5 = (bf16[288]{0:T(512)(128)(2,1)S(1)}, bf16[288]{0:T(512)(128)(2,1)}, u32[]{:S(2)}) copy-start(bf16[288]{0:T(512)(128)(2,1)} %param.17) | copy-start | bytes 1732

commit v2 on v1

v2 whole, which is shorter than its diff:
```python
import functools

import jax
import jax.numpy as jnp
from jax import lax
from jax.experimental import pallas as pl
from jax.experimental.pallas import tpu as pltpu
from jax.sharding import Mesh
from jax.sharding import PartitionSpec as P

DP = ("yl", "z", "c")
SECTION = ("yh", "x")
MESH_ID = pl.DeviceIdType.MESH

beta_first = 0.9
beta_second = 0.95
learn_rate = 0.002
decay_rate = 0.1
adam_eps = 1e-08
norm_eps = 1e-05
bias_first = 1.0 - 0.9**10
bias_second = 1.0 - 0.95**10


def remote(src, dst, send_sem, recv_sem, target):
    return pltpu.make_async_remote_copy(
        src_ref=src,
        dst_ref=dst,
        send_sem=send_sem,
        recv_sem=recv_sem,
        device_id=target,
        device_id_type=MESH_ID,
    )


def greet(targets):
    barrier = pltpu.get_barrier_semaphore()
    for target in targets:
        pl.semaphore_signal(barrier, inc=1, device_id=target, device_id_type=MESH_ID)
    pl.semaphore_wait(barrier, len(targets))


def lane_cuts(hidden):
    if hidden < 256:
        return [(0, hidden)]
    cut = (hidden // 256) * 128 + 128 * ((hidden // 128) % 2)
    return [(0, cut), (cut, hidden - cut)]


def new_weight(gradient, master_weight, adam_first, adam_second):
    first_new = beta_first * adam_first + (1.0 - beta_first) * gradient
    second_new = beta_second * adam_second + (1.0 - beta_second) * gradient * gradient
    update = first_new / bias_first / (jnp.sqrt(second_new / bias_second) + adam_eps)
    weight_new = master_weight - learn_rate * (update + decay_rate * master_weight)
    return weight_new, first_new, second_new


def kernel(
    nz,
    h_ref,
    o_ref,
    x_ref,
    state_refs,
    resid_ref,
    g_ref,
    out_ref,
    ot,
    hall,
    oall,
    part,
    sbuf,
    rbuf,
    state,
    xb,
    wall,
    pbuf,
    xbuf,
    ysend,
    ybuf,
    ss_out,
    ss_in,
    window,
    turned,
    h_send,
    h_recv,
    o_send,
    o_recv,
    r_send,
    r_recv,
    local_sem,
    p_send,
    p_recv,
    w_send,
    w_recv,
    c_send,
    c_recv,
    own_send,
    own_recv,
    x_send,
    x_recv,
    y_send,
    y_recv,
    s_send,
    s_recv,
):
    yl, z, c = lax.axis_index("yl"), lax.axis_index("z"), lax.axis_index("c")
    yh, x = lax.axis_index("yh"), lax.axis_index("x")
    steps = nz // 2
    tokens, hidden = h_ref.shape
    cols = ot.shape[3]
    half = cols // 2
    roll = x_ref.shape[0]
    per = 2 * nz // 8
    share = per * cols
    lanes = lane_cuts(hidden)
    pieces = range(len(lanes))
    core = {"c": 1 - c}
    across = {"yl": 1 - yl}
    diagonal = {"yl": 1 - yl, "c": 1 - c}
    ring = ({"z": lax.rem(z + 1, nz)}, {"z": lax.rem(z + nz - 1, nz)})
    place = yh * 4 + x
    section = []
    for r in range(1, 16):
        other = lax.rem(place + r, 16)
        section.append({"yh": other // 4, "x": lax.rem(other, 4)})
    flipped = [{"yl": 1 - yl, "yh": other} for other in range(4)]

    loads = []
    for i, ref in enumerate(state_refs):
        loads.append(pltpu.make_async_copy(ref, state.at[i], local_sem.at[i]))
    for i in range(2):
        base = (place * share + i * (share // 2)) // 128 * 128
        loads.append(
            pltpu.make_async_copy(
                resid_ref.at[:, pl.ds(pl.multiple_of(base, 128), 256)],
                window.at[pl.ds(i * roll, roll)],
                local_sem.at[4 + i],
            )
        )
    for load in loads:
        load.start()
    greet([core, diagonal, *ring, *section, *flipped])

    def h_copy(slot, n):
        first, width = lanes[n]
        spot = hall.at[pl.ds(slot * tokens, tokens), pl.ds(first, width)]
        source = h_ref.at[:, pl.ds(first, width)]
        if slot == 3:
            source = hall.at[pl.ds(2 * tokens, tokens), pl.ds(first, width)]
        return remote(
            source,
            spot,
            h_send.at[slot - 1, n],
            h_recv.at[slot - 1, n],
            across if slot == 2 else core,
        )

    def block_at(q):
        far = steps - (q + 1) // 2
        return lax.rem(jnp.where(q % 2 == 1, z + far, z + nz - far), nz)

    peers = [(1, core, yl, 1 - c), (2, across, 1 - yl, c), (3, diagonal, 1 - yl, 1 - c)]

    def o_copy(q, slot, target, to_yl, to_c):
        return remote(
            ot.at[to_yl, block_at(q), to_c],
            oall.at[q, :, pl.ds(slot * tokens, tokens)],
            o_send.at[slot - 1, q],
            o_recv.at[slot - 1, q],
            target,
        )

    def send_blocks(q, carry):
        for peer in peers:
            o_copy(q, *peer).start()
        oall[q, :, pl.ds(0, tokens)] = ot[yl, block_at(q), c]
        return carry

    h_copy(2, 0).start()
    h_copy(1, 0).start()

    def turn(i, carry):
        block = o_ref[:, pl.ds(pl.multiple_of(i * 4 * cols, 128), 4 * cols)]
        block = block.astype(jnp.float32).T.astype(jnp.bfloat16)
        pair_at = pl.ds(lax.rem(i, steps) * 2, 2)
        ot[i // steps, pair_at] = block.reshape(2, 2, cols, tokens)
        return carry

    lax.fori_loop(0, nz, turn, 0)
    send_blocks(0, 0)
    for n in pieces[1:]:
        h_copy(2, n).start()
        h_copy(1, n).start()
    lax.fori_loop(1, nz, send_blocks, 0)
    pair = remote(x_ref, xb.at[pl.ds(yl * roll, roll)], p_send.at[0], p_recv.at[0], across)
    pair.start()
    hall[pl.ds(0, tokens), :] = h_ref[...]
    xb[pl.ds(yl * roll, roll), :] = x_ref[...]

    def compute(q, slot, way, n):
        first, width = lanes[n]
        part[slot, way, :, pl.ds(first, width)] = jnp.dot(
            oall[q], hall[:, pl.ds(first, width)], preferred_element_type=jnp.float32
        )

    def arrived(q):
        for peer in peers:
            o_copy(q, *peer).wait_recv()

    def r_copy(way, sub, n, t):
        first, width = lanes[n]
        spot = (way, sub, t, slice(None), pl.ds(first, width))
        return remote(
            sbuf.at[spot],
            rbuf.at[spot],
            r_send.at[way, sub, n, t],
            r_recv.at[way, sub, n, t],
            ring[way],
        )

    def push(way, sub, n, t, slot, src_way, receive):
        first, width = lanes[n]
        value = part[slot, src_way, pl.ds(sub * half, half), pl.ds(first, width)]
        if receive:
            r_copy(way, sub, n, t - 1).wait_recv()
            value += rbuf[way, sub, t - 1, :, pl.ds(first, width)].astype(jnp.float32)
        sbuf[way, sub, t, :, pl.ds(first, width)] = value.astype(jnp.bfloat16)
        r_copy(way, sub, n, t).start()

    for n in pieces:
        h_copy(2, n).wait_recv()
        h_copy(3, n).start()
        h_copy(1, n).wait_recv()
        h_copy(3, n).wait_recv()
        if n == 0:
            arrived(0)
        compute(0, 0, 0, n)
        push(0, 0, n, 0, 0, 0, False)
        push(1, 1, n, 0, 0, 0, False)

    def fill(t):
        slot = lax.rem(t, 2)
        for way in range(2):
            arrived(2 * t - 1 + way)
            for n in pieces:
                compute(2 * t - 1 + way, slot, way, n)

    fill(1)
    for sub in range(2):
        for n in pieces:
            push(0, sub, n, 1, 1, 0, sub == 0)
            push(1, 1 - sub, n, 1, 1, 1, sub == 0)

    def step(t, carry):
        fill(t)
        slot = lax.rem(t, 2)
        for sub in range(2):
            for n in pieces:
                push(0, sub, n, t, slot, 0, True)
                push(1, 1 - sub, n, t, slot, 1, True)
        return carry

    lax.fori_loop(2, steps, step, 0)

    for load in loads:
        load.wait()
    turned[...] = window[...].astype(jnp.float32).T
    arrived(nz - 1)
    for n in pieces:
        compute(nz - 1, 0, 0, n)

    def w_copy(way, sub, n, t):
        first, width = lanes[n]
        block = lax.rem(z + nz - t, nz) if way == 0 else lax.rem(z + t, nz)
        spot = wall.at[block, c, pl.ds(sub * half, half), pl.ds(first, width)]
        return remote(
            spot, spot, w_send.at[way, sub, n, t], w_recv.at[way, sub, n, t], ring[way]
        )

    def c_copy(way, sub, n, t):
        first, width = lanes[n]
        block = lax.rem(z + 2 * nz - 1 - t, nz) if way == 0 else lax.rem(z + 1 + t, nz)
        spot = wall.at[block, c, pl.ds(sub * half, half), pl.ds(first, width)]
        return remote(spot, spot, c_send.at[way, sub, n, t], c_recv.at[way, sub, n, t], core)

    def own_copy(sub, n):
        first, width = lanes[n]
        spot = wall.at[z, c, pl.ds(sub * half, half), pl.ds(first, width)]
        return remote(spot, spot, own_send.at[sub, n], own_recv.at[sub, n], core)

    for sub in range(2):
        for n in pieces:
            first, width = lanes[n]
            here = (pl.ds(sub * half, half), pl.ds(first, width))
            value = part[0, 0, here[0], here[1]]
            for way in range(2):
                r_copy(way, sub, n, steps - 1).wait_recv()
                value += rbuf[way, sub, steps - 1, :, here[1]].astype(jnp.float32)
            g_ref[here] = value
            value += state[0, here[0], here[1]]
            weight, _, _ = new_weight(
                value,
                state[1, here[0], here[1]],
                state[2, here[0], here[1]],
                state[3, here[0], here[1]],
            )
            wall[z, c, here[0], here[1]] = weight.astype(jnp.bfloat16)
            for way in range(2):
                w_copy(way, sub, n, 0).start()
            own_copy(sub, n).start()

    def x_copy(rel, j, k):
        return remote(
            pbuf.at[j, k],
            xbuf.at[rel - 1, j // 4, k],
            x_send.at[rel - 1, j // 4, k],
            x_recv.at[rel - 1, j // 4, k],
            {"x": lax.rem(x + rel, 4)},
        )

    def multiply(block):
        product = lax.dot_general(
            wall[block].reshape(2 * cols, hidden),
            xb[...],
            (((1,), (1,)), ((), ())),
            preferred_element_type=jnp.float32,
        )
        for lane in range(2):
            piece = 2 * block + lane
            j, k = piece // per, lax.rem(piece, per)
            pbuf[j, k] = product[lane * cols : (lane + 1) * cols].astype(jnp.bfloat16)
            rel = lax.rem(lax.rem(j, 4) + 4 - x, 4)

            @pl.when(rel != 0)
            def _():
                x_copy(rel, j, k).start()

    def pass_on(t, short):
        for sub in range(2):
            for n in pieces:
                for way in range(2):
                    if way == sub:
                        w_copy(way, sub, n, t).wait_recv()
                        if short is not None:
                            w_copy(way, sub, n, t + 1).start()
                        c_copy(way, sub, n, t).start()
                    elif short is not None:
                        w_copy(way, sub, n, t).wait_recv()
                        if short:
                            w_copy(way, sub, n, t + 1).start()
                        c_copy(way, sub, n, t).start()

    def multiply_step(t):
        for way in range(2):
            for sub in range(2):
                for n in pieces:
                    c_copy(way, sub, n, t).wait_recv()
            multiply(lax.rem(z + nz - 1 - t, nz) if way == 0 else lax.rem(z + 1 + t, nz))

    pair.wait_recv()
    pass_on(0, steps > 2)
    for sub in range(2):
        for n in pieces:
            own_copy(sub, n).wait_recv()
    multiply(z)

    def w_step(t, carry):
        pass_on(t, True)
        multiply_step(t - 1)
        return carry

    lax.fori_loop(1, steps - 2, w_step, 0)
    if steps > 2:
        pass_on(steps - 2, False)
        multiply_step(steps - 3)
    pass_on(steps - 1, None)
    multiply_step(steps - 2)
    for n in pieces:
        for way in range(2):
            c_copy(way, way, n, steps - 1).wait_recv()
    multiply(lax.rem(z + steps, nz))

    def y_copy(to_yl, jj):
        return remote(
            ysend.at[to_yl, jj],
            ybuf.at[yh],
            y_send.at[to_yl, jj],
            y_recv.at[yh],
            {"yl": to_yl, "yh": 2 * yl + jj},
        )

    for jj in range(2):
        total = pbuf[jj * 4 + x].astype(jnp.float32)
        for rel in range(1, 4):
            for k in range(per):
                x_copy(rel, jj * 4, k).wait_recv()
            total += xbuf[rel - 1, jj].astype(jnp.float32)
        total = total.reshape(share, 2 * roll)
        for to_yl in range(2):
            rows = slice(to_yl * roll, (to_yl + 1) * roll)
            packed = jnp.concatenate(
                [total[: share // 2, rows], total[share // 2 :, rows]], axis=1
            ).astype(jnp.bfloat16)
            mine = jnp.logical_and(yl == to_yl, yh == 2 * yl + jj)

            @pl.when(mine)
            def _(packed=packed):
                ybuf[yh] = packed

            @pl.when(jnp.logical_not(mine))
            def _(packed=packed, to_yl=to_yl, jj=jj):
                ysend[to_yl, jj] = packed
                y_copy(to_yl, jj).start()

    halves = []
    for i in range(2):
        shift = lax.rem(place * share + i * (share // 2), 128)
        halves.append(turned[pl.ds(pl.multiple_of(shift, 8), share // 2), :])
    lane_at = lax.broadcasted_iota(jnp.int32, (share // 2, 2 * roll), 1)
    stream = jnp.where(lane_at < roll, halves[0], halves[1])
    for source in range(4):
        mine = jnp.logical_and(yh == source, yh // 2 == yl)

        @pl.when(jnp.logical_not(mine))
        def _(source=source):
            remote(
                ysend.at[0, 0], ybuf.at[source], y_send.at[0, 0], y_recv.at[source], across
            ).wait_recv()

        stream += ybuf[source].astype(jnp.float32)

    square = jnp.sum(stream * stream, axis=0, keepdims=True)
    square = jnp.broadcast_to(square, (8, 2 * roll))
    square = square + pltpu.roll(square, roll, 1)
    ss_out[...] = square

    def s_copy(r):
        return remote(ss_out, ss_in.at[r - 1], s_send.at[r - 1], s_recv.at[r - 1], section[r - 1])

    for r in range(1, 16):
        s_copy(r).start()
    for r in range(1, 16):
        s_copy(r).wait_recv()
        square += ss_in[r - 1]
    scale = lax.rsqrt(square * (1.0 / (16 * share)) + norm_eps)
    out_ref[...] = stream * scale[0:1]

    pair.wait_send()
    for slot in range(1, 4):
        for n in pieces:
            h_copy(slot, n).wait_send()

    def drain_blocks(q, carry):
        for peer in peers:
            o_copy(q, *peer).wait_send()
        return carry

    lax.fori_loop(0, nz, drain_blocks, 0)
    for n in pieces:
        r_copy(0, 0, n, 0).wait_send()
        r_copy(1, 1, n, 0).wait_send()
        for sub in range(2):
            own_copy(sub, n).wait_send()
            w_copy(sub, sub, n, steps - 1).wait_send()
            c_copy(sub, sub, n, steps - 1).wait_send()

    def drain(t, carry):
        for way in range(2):
            for sub in range(2):
                for n in pieces:
                    r_copy(way, sub, n, t + 1).wait_send()
                    w_copy(way, sub, n, t).wait_send()
                    c_copy(way, sub, n, t).wait_send()
        return carry

    lax.fori_loop(0, steps - 1, drain, 0)
    for rel in range(1, 4):
        for jj in range(2):
            for k in range(per):
                x_copy(rel, jj * 4, k).wait_send()
    for jj in range(2):
        for to_yl in range(2):
            mine = jnp.logical_and(yl == to_yl, yh == 2 * yl + jj)

            @pl.when(jnp.logical_not(mine))
            def _(to_yl=to_yl, jj=jj):
                y_copy(to_yl, jj).wait_send()

    for r in range(1, 16):
        s_copy(r).wait_send()


def update_and_decode(nz, hidden_act, out_grad, flat_in, state, resid):
    tokens, hidden = hidden_act.shape
    cols = state[0].shape[0]
    roll = flat_in.shape[0]
    steps = nz // 2
    per = 2 * nz // 8
    middle = per * cols // 2
    vmem = pl.BlockSpec(memory_space=pltpu.VMEM)
    hbm = pl.BlockSpec(memory_space=pl.ANY)
    dma = pltpu.SemaphoreType.DMA
    links = [dma((2, 2, 2, steps))] * 2
    return pl.pallas_call(
        functools.partial(kernel, nz),
        out_shape=(
            jax.ShapeDtypeStruct((cols, hidden), jnp.float32),
            jax.ShapeDtypeStruct((middle, 2 * roll), jnp.float32),
        ),
        in_specs=[vmem, vmem, vmem, [hbm] * 4, hbm],
        out_specs=(vmem, vmem),
        scratch_shapes=[
            pltpu.VMEM((2, nz, 2, cols, tokens), jnp.bfloat16),
            pltpu.VMEM((4 * tokens, hidden), jnp.bfloat16),
            pltpu.VMEM((nz, cols, 4 * tokens), jnp.bfloat16),
            pltpu.VMEM((2, 2, cols, hidden), jnp.float32),
            pltpu.VMEM((2, 2, steps, cols // 2, hidden), jnp.bfloat16),
            pltpu.VMEM((2, 2, steps, cols // 2, hidden), jnp.bfloat16),
            pltpu.VMEM((4, cols, hidden), jnp.float32),
            pltpu.VMEM((2 * roll, hidden), jnp.bfloat16),
            pltpu.VMEM((nz, 2, cols, hidden), jnp.bfloat16),
            pltpu.VMEM((8, per, cols, 2 * roll), jnp.bfloat16),
            pltpu.VMEM((3, 2, per, cols, 2 * roll), jnp.bfloat16),
            pltpu.VMEM((2, 2, middle, 2 * roll), jnp.bfloat16),
            pltpu.VMEM((4, middle, 2 * roll), jnp.bfloat16),
            pltpu.VMEM((8, 2 * roll), jnp.float32),
            pltpu.VMEM((15, 8, 2 * roll), jnp.float32),
            pltpu.VMEM((2 * roll, 256), jnp.bfloat16),
            pltpu.VMEM((256, 2 * roll), jnp.float32),
            dma((3, 2)),
            dma((3, 2)),
            dma((3, nz)),
            dma((3, nz)),
            *links,
            dma((6,)),
            dma((1,)),
            dma((1,)),
            *links,
            *links,
            dma((2, 2)),
            dma((2, 2)),
            dma((3, 2, per)),
            dma((3, 2, per)),
            dma((2, 2)),
            dma((4,)),
            dma((15,)),
            dma((15,)),
        ],
        compiler_params=pltpu.CompilerParams(collective_id=0, has_side_effects=True),
        cost_estimate=pl.CostEstimate(
            flops=8 * nz * cols * hidden * (tokens + roll),
            bytes_accessed=3000000,
            transcendentals=0,
        ),
        name="update_and_decode",
    )(hidden_act, out_grad, flat_in, list(state), resid)


def per_device(
    hidden_act,
    out_grad,
    grad_accum,
    master_weight,
    adam_first,
    adam_second,
    decode_in,
    residual_in,
    norm_gain,
):
    nz = lax.axis_size("z")
    steps_count, roll_rows, hidden_local = decode_in.shape
    flat_rows = steps_count * roll_rows
    flat_in = decode_in.reshape(flat_rows, hidden_local)
    resid_flat = residual_in.reshape(flat_rows, -1)
    state = (grad_accum.T, master_weight.T, adam_first.T, adam_second.T)
    grad_share, packed = update_and_decode(
        nz, hidden_act, out_grad, flat_in, state, resid_flat
    )
    weight_new, first_new, second_new = new_weight(
        grad_share.T + grad_accum, master_weight, adam_first, adam_second
    )
    normed = jnp.concatenate([packed[:, :flat_rows], packed[:, flat_rows:]], axis=0).T
    decoded = (normed * norm_gain.astype(jnp.float32)).astype(jnp.bfloat16)
    decoded = decoded.reshape(steps_count, roll_rows, -1)
    return (weight_new, first_new, second_new, decoded)


def solution(mesh):
    finer = Mesh(mesh.devices.reshape(2, 12, 2, 4, 4), ("yl", "z", "c", "yh", "x"))
    in_specs = (
        P(DP, SECTION),
        P(DP, None),
        P(SECTION, DP),
        P(SECTION, DP),
        P(SECTION, DP),
        P(SECTION, DP),
        P(None, DP, SECTION),
        P(None, DP, None),
        P(SECTION),
    )
    out_specs = (P(SECTION, DP), P(SECTION, DP), P(SECTION, DP), P(None, DP, SECTION))
    return jax.shard_map(
        per_device, mesh=finer, in_specs=in_specs, out_specs=out_specs, check_vma=False
    )
```

time: 112 us -> 105 us (0.938)
  Pallas kernels: 103 us -> 98.3 us
  local copies, waits for them, and re-layouts: 4.56 us -> 1.77 us
    pallas_call x2 -> x1, Pallas kernels: 103 us -> 98.3 us  [update_and_decode(): pl.pallas_call(functools.partial(kernel, nz), out_shape=(jax.ShapeDtypeSt...]
    transpose x2 -> x0, local copies, waits for them, and re-layouts: 3.16 us -> none  [the longest x1 2.44 us: per_device(): out_t = out_grad.T.reshape(2, nz, 2, rows, tokens)]
    transpose x3 -> x0, other arithmetic: 2.2 us -> none  [the longest x1 2.17 us: per_device(): packed = decode(nz, weight_rounded.T, flat_in, resid, gain)]
    sub x0 -> x1, other arithmetic: none -> 2.11 us  [new_weight(): master_weight - learn_rate * (update + decay_rate * master_weight)]
where the time goes in v2:
time: 105 us; the launch traced here: 104 us
  Pallas kernels  98.3 us (94%)
  other arithmetic  2.9 us (3%)
  local copies, waits for them, and re-layouts  1.77 us (2%)
    pallas_call x1, Pallas kernels, update_and_decode(): pl.pallas_call(functools.partial(kernel, nz), out_shape=(jax.ShapeDtypeSt...  98.3 us
    sub x1, other arithmetic, new_weight(): master_weight - learn_rate * (update + decay_rate * master_weight)  2.11 us

profile of v2, /device:TPU:6, one launch (start us, length us, event | category | flops | bytes accessed | tf_op | source)
XLA Modules:
  0.0 103.6 jit_solution(5984466965314992157)
XLA Ops:
  0.6 0.7 convert_element_type.9
  1.3 0.0 copy-start
  1.3 0.0 copy-start.1
  1.3 0.0 copy-start.2
  1.3 0.0 copy-start.3
  1.3 98.3 %update_and_decode.1 = (f32[96,896]{1,0:T(8,128)}, f32[144,128]{1,0:T(8,128)}) custom-call(bf16[128,896]{1,0:T(8,128)(2,1)} %h_ref.1, bf16[128,4608]{1,0:T(8,128)(2,1)} %o_ref.1, bf16[64,896]{1,0:T(8,128)(2,1)} %bitcast.23, f32[96,896]{1,0:T(8,128)} %bitcast.18, f32[96,896]{1,0:T(8,128)} %bitcast.17, f32[96,896]{1,0:T(8,128)} %bitcast.19, ...), custom_call_target="tpu_custom_call" | custom-call | flops 1585446912 | bytes 3000000 | tf_op jit(solution)/shard_map/update_and_decode/pallas_call | solution.py:504
  99.6 1.0 %fusion.4 = (f32[144,64]{1,0:T(8,128)S(1)}, f32[144,64]{1,0:T(8,128)S(1)}) fusion(f32[144,128]{1,0:T(8,128)} %get-tuple-element.7), kind=kLoop, calls=%fused_computation.8 | loop fusion | bytes 147456 | tf_op jit(solution)/shard_map/slice | solution.py:582
  100.7 0.1 fusion.2
  100.8 0.7 copy.14
  101.5 0.0 copy-done
  101.5 0.0 copy-done.1
  101.5 0.0 copy-done.2
  101.5 0.0 copy-done.3
  101.5 2.1 %multiply_subtract_fusion = (f32[896,96]{0,1:T(8,128)}, f32[896,96]{0,1:T(8,128)}, f32[896,96]{0,1:T(8,128)}) fusion(f32[896,96]{0,1:T(8,128)S(1)} %copy-done, f32[896,96]{0,1:T(8,128)S(1)} %copy-done.1, f32[96,896]{1,0:T(8,128)} %get-tuple-element.6, f32[896,96]{0,1:T(8,128)S(1)} %copy-done.2, f32[896,96]{0,1:T(8,128)S(1)} %copy-done.3), kind=kLoop, calls=%fused_computation.3 | loop fusion | flops 1376256 | bytes 2752512 | tf_op jit(solution)/shard_map/sub | solution.py:54
Async XLA Ops:
  1.3 100.2 %copy-start = (f32[896,96]{0,1:T(8,128)S(1)}, f32[896,96]{0,1:T(8,128)}, u32[]{:S(2)}) copy-start(f32[896,96]{0,1:T(8,128)} %param.12) | copy-start | bytes 1032196
  1.3 100.2 %copy-start.1 = (f32[896,96]{0,1:T(8,128)S(1)}, f32[896,96]{0,1:T(8,128)}, u32[]{:S(2)}) copy-start(f32[896,96]{0,1:T(8,128)} %param.11) | copy-start | bytes 1032196
  1.3 100.2 %copy-start.2 = (f32[896,96]{0,1:T(8,128)S(1)}, f32[896,96]{0,1:T(8,128)}, u32[]{:S(2)}) copy-start(f32[896,96]{0,1:T(8,128)} %param.13) | copy-start | bytes 1032196
  1.3 100.2 %copy-start.3 = (f32[896,96]{0,1:T(8,128)S(1)}, f32[896,96]{0,1:T(8,128)}, u32[]{:S(2)}) copy-start(f32[896,96]{0,1:T(8,128)} %param.14) | copy-start | bytes 1032196

commit v3 on v2

--- a/solution.py
+++ b/solution.py
@@ -43,7 +43,7 @@
 def lane_cuts(hidden):
     if hidden < 256:
         return [(0, hidden)]
-    cut = (hidden // 256) * 128 + 128 * ((hidden // 128) % 2)
+    cut = (hidden // 256) * 128
     return [(0, cut), (cut, hidden - cut)]
 
 
@@ -62,8 +62,10 @@
     x_ref,
     state_refs,
     resid_ref,
+    gain_ref,
     g_ref,
     out_ref,
+    o_vm,
     ot,
     hall,
     oall,
@@ -125,14 +127,25 @@
         section.append({"yh": other // 4, "x": lax.rem(other, 4)})
     flipped = [{"yl": 1 - yl, "yh": other} for other in range(4)]
 
+    width = o_ref.shape[1] // 3
+    o_loads = []
+    for i in range(3):
+        part_at = (slice(None), pl.ds(i * width, width))
+        o_loads.append(pltpu.make_async_copy(o_ref.at[part_at], o_vm.at[part_at], local_sem.at[6 + i]))
+        o_loads[i].start()
     loads = []
     for i, ref in enumerate(state_refs):
         loads.append(pltpu.make_async_copy(ref, state.at[i], local_sem.at[i]))
+    span = window.shape[1]
+    shifts = []
     for i in range(2):
-        base = (place * share + i * (share // 2)) // 128 * 128
+        first_col = place * share + i * half
+        base = first_col // 128 * 128
+        base = jnp.where(base > 16 * share - span, 16 * share - span, base)
+        shifts.append(first_col - base)
         loads.append(
             pltpu.make_async_copy(
-                resid_ref.at[:, pl.ds(pl.multiple_of(base, 128), 256)],
+                resid_ref.at[:, pl.ds(pl.multiple_of(base, 128), span)],
                 window.at[pl.ds(i * roll, roll)],
                 local_sem.at[4 + i],
             )
@@ -180,13 +193,15 @@
     h_copy(1, 0).start()
 
     def turn(i, carry):
-        block = o_ref[:, pl.ds(pl.multiple_of(i * 4 * cols, 128), 4 * cols)]
+        block = o_vm[:, pl.ds(pl.multiple_of(i * 4 * cols, 128), 4 * cols)]
         block = block.astype(jnp.float32).T.astype(jnp.bfloat16)
         pair_at = pl.ds(lax.rem(i, steps) * 2, 2)
         ot[i // steps, pair_at] = block.reshape(2, 2, cols, tokens)
         return carry
 
-    lax.fori_loop(0, nz, turn, 0)
+    for i in range(3):
+        o_loads[i].wait()
+        lax.fori_loop(i * nz // 3, (i + 1) * nz // 3, turn, 0)
     send_blocks(0, 0)
     for n in pieces[1:]:
         h_copy(2, n).start()
@@ -246,16 +261,16 @@
                 compute(2 * t - 1 + way, slot, way, n)
 
     fill(1)
-    for sub in range(2):
-        for n in pieces:
+    for n in pieces:
+        for sub in range(2):
             push(0, sub, n, 1, 1, 0, sub == 0)
             push(1, 1 - sub, n, 1, 1, 1, sub == 0)
 
     def step(t, carry):
         fill(t)
         slot = lax.rem(t, 2)
-        for sub in range(2):
-            for n in pieces:
+        for n in pieces:
+            for sub in range(2):
                 push(0, sub, n, t, slot, 0, True)
                 push(1, 1 - sub, n, t, slot, 1, True)
         return carry
@@ -288,8 +303,8 @@
         spot = wall.at[z, c, pl.ds(sub * half, half), pl.ds(first, width)]
         return remote(spot, spot, own_send.at[sub, n], own_recv.at[sub, n], core)
 
-    for sub in range(2):
-        for n in pieces:
+    for n in pieces:
+        for sub in range(2):
             first, width = lanes[n]
             here = (pl.ds(sub * half, half), pl.ds(first, width))
             value = part[0, 0, here[0], here[1]]
@@ -335,9 +350,50 @@
             def _():
                 x_copy(rel, j, k).start()
 
+    def y_copy(to_yl, jj, k):
+        return remote(
+            ysend.at[to_yl, jj, k],
+            ybuf.at[yh, k],
+            y_send.at[to_yl, jj, k],
+            y_recv.at[yh, k],
+            {"yl": to_yl, "yh": 2 * yl + jj},
+        )
+
+    def finish(block):
+        for lane in range(2):
+            piece = 2 * block + lane
+            j, k = piece // per, lax.rem(piece, per)
+            jj = j // 4
+
+            @pl.when(lax.rem(j, 4) == x)
+            def _(j=j, k=k, jj=jj):
+                total = pbuf[j, k].astype(jnp.float32)
+                for rel in range(1, 4):
+                    x_copy(rel, j, k).wait_recv()
+                    total += xbuf[rel - 1, jj, k].astype(jnp.float32)
+                for to_yl in range(2):
+                    rows = slice(to_yl * roll, (to_yl + 1) * roll)
+                    packed = jnp.concatenate(
+                        [total[:half, rows], total[half:, rows]], axis=1
+                    ).astype(jnp.bfloat16)
+                    mine = jnp.logical_and(yl == to_yl, yh == 2 * yl + jj)
+
+                    @pl.when(mine)
+                    def _(packed=packed):
+                        ybuf[yh, k] = packed
+
+                    @pl.when(jnp.logical_not(mine))
+                    def _(packed=packed, to_yl=to_yl):
+                        ysend[to_yl, jj, k] = packed
+                        y_copy(to_yl, jj, k).start()
+
+    def finish_step(t):
+        finish(lax.rem(z + nz - 1 - t, nz))
+        finish(lax.rem(z + 1 + t, nz))
+
     def pass_on(t, short):
-        for sub in range(2):
-            for n in pieces:
+        for n in pieces:
+            for sub in range(2):
                 for way in range(2):
                     if way == sub:
                         w_copy(way, sub, n, t).wait_recv()
@@ -364,70 +420,59 @@
             own_copy(sub, n).wait_recv()
     multiply(z)
 
-    def w_step(t, carry):
-        pass_on(t, True)
-        multiply_step(t - 1)
-        return carry
-
-    lax.fori_loop(1, steps - 2, w_step, 0)
-    if steps > 2:
+    if steps > 3:
+        pass_on(1, True)
+        multiply_step(0)
+        finish(z)
+
+        def w_step(t, carry):
+            pass_on(t, True)
+            multiply_step(t - 1)
+            finish_step(t - 2)
+            return carry
+
+        lax.fori_loop(2, steps - 2, w_step, 0)
         pass_on(steps - 2, False)
         multiply_step(steps - 3)
-    pass_on(steps - 1, None)
-    multiply_step(steps - 2)
+        finish_step(steps - 4)
+        pass_on(steps - 1, None)
+        multiply_step(steps - 2)
+        finish_step(steps - 3)
+    else:
+        pass_on(steps - 1, None)
+        multiply_step(steps - 2)
+        finish(z)
     for n in pieces:
         for way in range(2):
             c_copy(way, way, n, steps - 1).wait_recv()
     multiply(lax.rem(z + steps, nz))
-
-    def y_copy(to_yl, jj):
-        return remote(
-            ysend.at[to_yl, jj],
-            ybuf.at[yh],
-            y_send.at[to_yl, jj],
-            y_recv.at[yh],
-            {"yl": to_yl, "yh": 2 * yl + jj},
-        )
-
-    for jj in range(2):
-        total = pbuf[jj * 4 + x].astype(jnp.float32)
-        for rel in range(1, 4):
-            for k in range(per):
-                x_copy(rel, jj * 4, k).wait_recv()
-            total += xbuf[rel - 1, jj].astype(jnp.float32)
-        total = total.reshape(share, 2 * roll)
-        for to_yl in range(2):
-            rows = slice(to_yl * roll, (to_yl + 1) * roll)
-            packed = jnp.concatenate(
-                [total[: share // 2, rows], total[share // 2 :, rows]], axis=1
-            ).astype(jnp.bfloat16)
-            mine = jnp.logical_and(yl == to_yl, yh == 2 * yl + jj)
-
-            @pl.when(mine)
-            def _(packed=packed):
-                ybuf[yh] = packed
-
-            @pl.when(jnp.logical_not(mine))
-            def _(packed=packed, to_yl=to_yl, jj=jj):
-                ysend[to_yl, jj] = packed
-                y_copy(to_yl, jj).start()
-
-    halves = []
-    for i in range(2):
-        shift = lax.rem(place * share + i * (share // 2), 128)
-        halves.append(turned[pl.ds(pl.multiple_of(shift, 8), share // 2), :])
-    lane_at = lax.broadcasted_iota(jnp.int32, (share // 2, 2 * roll), 1)
-    stream = jnp.where(lane_at < roll, halves[0], halves[1])
+    finish_step(steps - 2)
+    finish(lax.rem(z + steps, nz))
+
+    lane_at = lax.broadcasted_iota(jnp.int32, (half, 2 * roll), 1)
+    streams = []
+    for k in range(per):
+        left, right = [
+            turned[pl.ds(pl.multiple_of(shift + k * cols, 8), half), :] for shift in shifts
+        ]
+        streams.append(jnp.where(lane_at < roll, left, right))
     for source in range(4):
         mine = jnp.logical_and(yh == source, yh // 2 == yl)
 
         @pl.when(jnp.logical_not(mine))
         def _(source=source):
-            remote(
-                ysend.at[0, 0], ybuf.at[source], y_send.at[0, 0], y_recv.at[source], across
-            ).wait_recv()
-
-        stream += ybuf[source].astype(jnp.float32)
+            for k in range(per):
+                remote(
+                    ysend.at[0, 0, 0],
+                    ybuf.at[source, k],
+                    y_send.at[0, 0, 0],
+                    y_recv.at[source, k],
+                    across,
+                ).wait_recv()
+
+        for k in range(per):
+            streams[k] += ybuf[source, k].astype(jnp.float32)
+    stream = jnp.concatenate(streams, axis=0)
 
     square = jnp.sum(stream * stream, axis=0, keepdims=True)
     square = jnp.broadcast_to(square, (8, 2 * roll))
@@ -443,7 +488,13 @@
         s_copy(r).wait_recv()
         square += ss_in[r - 1]
     scale = lax.rsqrt(square * (1.0 / (16 * share)) + norm_eps)
-    out_ref[...] = stream * scale[0:1]
+    normed = (stream * scale[0:1]).T
+    natural = []
+    for k in range(per):
+        for i in range(2):
+            natural.append(normed[i * roll : (i + 1) * roll, k * half : (k + 1) * half])
+    natural = jnp.concatenate(natural, axis=1)
+    out_ref[...] = (natural * gain_ref[...].astype(jnp.float32)).astype(jnp.bfloat16)
 
     pair.wait_send()
     for slot in range(1, 4):
@@ -484,19 +535,22 @@
 
             @pl.when(jnp.logical_not(mine))
             def _(to_yl=to_yl, jj=jj):
-                y_copy(to_yl, jj).wait_send()
+                for k in range(per):
+                    y_copy(to_yl, jj, k).wait_send()
 
     for r in range(1, 16):
         s_copy(r).wait_send()
 
 
-def update_and_decode(nz, hidden_act, out_grad, flat_in, state, resid):
+def update_and_decode(nz, hidden_act, out_grad, flat_in, state, resid, gain):
     tokens, hidden = hidden_act.shape
     cols = state[0].shape[0]
     roll = flat_in.shape[0]
     steps = nz // 2
     per = 2 * nz // 8
-    middle = per * cols // 2
+    half = cols // 2
+    share = per * cols
+    span = (2 * cols + half + 112 + 127) // 128 * 128
     vmem = pl.BlockSpec(memory_space=pltpu.VMEM)
     hbm = pl.BlockSpec(memory_space=pl.ANY)
     dma = pltpu.SemaphoreType.DMA
@@ -505,11 +559,12 @@
         functools.partial(kernel, nz),
         out_shape=(
             jax.ShapeDtypeStruct((cols, hidden), jnp.float32),
-            jax.ShapeDtypeStruct((middle, 2 * roll), jnp.float32),
+            jax.ShapeDtypeStruct((roll, share), jnp.bfloat16),
         ),
-        in_specs=[vmem, vmem, vmem, [hbm] * 4, hbm],
+        in_specs=[vmem, hbm, vmem, [hbm] * 4, hbm, vmem],
         out_specs=(vmem, vmem),
         scratch_shapes=[
+            pltpu.VMEM(out_grad.shape, jnp.bfloat16),
             pltpu.VMEM((2, nz, 2, cols, tokens), jnp.bfloat16),
             pltpu.VMEM((4 * tokens, hidden), jnp.bfloat16),
             pltpu.VMEM((nz, cols, 4 * tokens), jnp.bfloat16),
@@ -521,18 +576,18 @@
             pltpu.VMEM((nz, 2, cols, hidden), jnp.bfloat16),
             pltpu.VMEM((8, per, cols, 2 * roll), jnp.bfloat16),
             pltpu.VMEM((3, 2, per, cols, 2 * roll), jnp.bfloat16),
-            pltpu.VMEM((2, 2, middle, 2 * roll), jnp.bfloat16),
-            pltpu.VMEM((4, middle, 2 * roll), jnp.bfloat16),
+            pltpu.VMEM((2, 2, per, half, 2 * roll), jnp.bfloat16),
+            pltpu.VMEM((4, per, half, 2 * roll), jnp.bfloat16),
             pltpu.VMEM((8, 2 * roll), jnp.float32),
             pltpu.VMEM((15, 8, 2 * roll), jnp.float32),
-            pltpu.VMEM((2 * roll, 256), jnp.bfloat16),
-            pltpu.VMEM((256, 2 * roll), jnp.float32),
+            pltpu.VMEM((2 * roll, span), jnp.bfloat16),
+            pltpu.VMEM((span, 2 * roll), jnp.float32),
             dma((3, 2)),
             dma((3, 2)),
             dma((3, nz)),
             dma((3, nz)),
             *links,
-            dma((6,)),
+            dma((9,)),
             dma((1,)),
             dma((1,)),
             *links,
@@ -541,8 +596,8 @@
             dma((2, 2)),
             dma((3, 2, per)),
             dma((3, 2, per)),
-            dma((2, 2)),
-            dma((4,)),
+            dma((2, 2, per)),
+            dma((4, per)),
             dma((15,)),
             dma((15,)),
         ],
@@ -553,7 +608,7 @@
             transcendentals=0,
         ),
         name="update_and_decode",
-    )(hidden_act, out_grad, flat_in, list(state), resid)
+    )(hidden_act, out_grad, flat_in, list(state), resid, gain)
 
 
 def per_device(
@@ -573,14 +628,12 @@
     flat_in = decode_in.reshape(flat_rows, hidden_local)
     resid_flat = residual_in.reshape(flat_rows, -1)
     state = (grad_accum.T, master_weight.T, adam_first.T, adam_second.T)
-    grad_share, packed = update_and_decode(
-        nz, hidden_act, out_grad, flat_in, state, resid_flat
+    grad_share, decoded = update_and_decode(
+        nz, hidden_act, out_grad, flat_in, state, resid_flat, norm_gain[None]
     )
     weight_new, first_new, second_new = new_weight(
         grad_share.T + grad_accum, master_weight, adam_first, adam_second
     )
-    normed = jnp.concatenate([packed[:, :flat_rows], packed[:, flat_rows:]], axis=0).T
-    decoded = (normed * norm_gain.astype(jnp.float32)).astype(jnp.bfloat16)
     decoded = decoded.reshape(steps_count, roll_rows, -1)
     return (weight_new, first_new, second_new, decoded)
 

time: 105 us -> 102 us (0.971)
  Pallas kernels: 98.3 us -> 96.7 us
    pallas_call x1, Pallas kernels: 98.3 us -> 96.7 us  [update_and_decode(): pl.pallas_call(functools.partial(kernel, nz), out_shape=(jax.ShapeDtypeSt...]
    broadcast_in_dim x0 -> x1, local copies, waits for them, and re-layouts: none -> 1.24 us  [per_device(): norm_gain[None]]
where the time goes in v3:
time: 102 us; the launch traced here: 101 us
  Pallas kernels  96.7 us (95%)
  other arithmetic  2.12 us (2%)
  local copies, waits for them, and re-layouts  1.88 us (2%)
    pallas_call x1, Pallas kernels, update_and_decode(): pl.pallas_call(functools.partial(kernel, nz), out_shape=(jax.ShapeDtypeSt...  96.7 us
    sub x1, other arithmetic, new_weight(): master_weight - learn_rate * (update + decay_rate * master_weight)  2.12 us

profile of v3, /device:TPU:6, one launch (start us, length us, event | category | flops | bytes accessed | tf_op | source)
XLA Modules:
  0.0 101.4 jit_solution(1869463003764695634)
XLA Ops:
  0.6 1.2 %broadcast_in_dim.3.gain_ref = bf16[1,288]{1,0:T(2,128)(2,1)} reshape(bf16[288]{0:T(512)(128)(2,1)} %param.17) | data formatting | bytes 1152 | tf_op jit(solution)/shard_map/broadcast_in_dim | solution.py:632
  1.9 0.0 copy-start
  1.9 0.0 copy-start.1
  1.9 0.0 copy-start.2
  1.9 0.0 copy-start.3
  1.9 96.7 %update_and_decode.1 = (f32[96,896]{1,0:T(8,128)}, bf16[64,288]{1,0:T(8,128)(2,1)}) custom-call(bf16[128,896]{1,0:T(8,128)(2,1)} %h_ref.1, bf16[128,4608]{1,0:T(8,128)(2,1)} %o_ref.1, bf16[64,896]{1,0:T(8,128)(2,1)} %bitcast.21, f32[96,896]{1,0:T(8,128)} %bitcast.16, f32[96,896]{1,0:T(8,128)} %bitcast.15, f32[96,896]{1,0:T(8,128)} %bitcast.17, ...), custom_call_target="tpu_custom_call" | custom-call | flops 1585446912 | bytes 3000000 | tf_op jit(solution)/shard_map/update_and_decode/pallas_call | solution.py:558
  98.6 0.0 copy-done
  98.6 0.0 copy-done.1
  98.6 0.0 copy-done.2
  98.6 0.0 copy-done.3
  98.6 0.0 copy-start.4
  98.6 2.1 %multiply_subtract_fusion = (f32[896,96]{0,1:T(8,128)}, f32[896,96]{0,1:T(8,128)}, f32[896,96]{0,1:T(8,128)}) fusion(f32[896,96]{0,1:T(8,128)S(1)} %copy-done, f32[896,96]{0,1:T(8,128)S(1)} %copy-done.1, f32[96,896]{1,0:T(8,128)} %get-tuple-element.6, f32[896,96]{0,1:T(8,128)S(1)} %copy-done.2, f32[896,96]{0,1:T(8,128)S(1)} %copy-done.3), kind=kLoop, calls=%fused_computation.3 | loop fusion | flops 1376256 | bytes 2752512 | tf_op jit(solution)/shard_map/sub | solution.py:54
  100.7 0.0 copy-done.4
  100.7 0.6 copy.14
Async XLA Ops:
  1.9 96.7 %copy-start = (f32[896,96]{0,1:T(8,128)S(1)}, f32[896,96]{0,1:T(8,128)}, u32[]{:S(2)}) copy-start(f32[896,96]{0,1:T(8,128)} %param.12) | copy-start | bytes 1032196
  1.9 96.7 %copy-start.1 = (f32[896,96]{0,1:T(8,128)S(1)}, f32[896,96]{0,1:T(8,128)}, u32[]{:S(2)}) copy-start(f32[896,96]{0,1:T(8,128)} %param.11) | copy-start | bytes 1032196
  1.9 96.7 %copy-start.2 = (f32[896,96]{0,1:T(8,128)S(1)}, f32[896,96]{0,1:T(8,128)}, u32[]{:S(2)}) copy-start(f32[896,96]{0,1:T(8,128)} %param.13) | copy-start | bytes 1032196
  1.9 96.7 %copy-start.3 = (f32[896,96]{0,1:T(8,128)S(1)}, f32[896,96]{0,1:T(8,128)}, u32[]{:S(2)}) copy-start(f32[896,96]{0,1:T(8,128)} %param.14) | copy-start | bytes 1032196
  98.6 2.1 %copy-start.4 = (bf16[64,288]{1,0:T(8,128)(2,1)S(1)}, bf16[64,288]{1,0:T(8,128)(2,1)}, u32[]{:S(2)}) copy-start(bf16[64,288]{1,0:T(8,128)(2,1)} %get-tuple-element.7) | copy-start | bytes 110596

commit v4 on v3

--- a/solution.py
+++ b/solution.py
@@ -62,9 +62,10 @@
     x_ref,
     state_refs,
     resid_ref,
-    gain_ref,
     g_ref,
     out_ref,
+    h_vm,
+    x_vm,
     o_vm,
     ot,
     hall,
@@ -127,12 +128,16 @@
         section.append({"yh": other // 4, "x": lax.rem(other, 4)})
     flipped = [{"yl": 1 - yl, "yh": other} for other in range(4)]
 
+    h_load = pltpu.make_async_copy(h_ref, h_vm, local_sem.at[9])
+    x_load = pltpu.make_async_copy(x_ref, x_vm, local_sem.at[10])
+    h_load.start()
     width = o_ref.shape[1] // 3
     o_loads = []
     for i in range(3):
         part_at = (slice(None), pl.ds(i * width, width))
         o_loads.append(pltpu.make_async_copy(o_ref.at[part_at], o_vm.at[part_at], local_sem.at[6 + i]))
         o_loads[i].start()
+    x_load.start()
     loads = []
     for i, ref in enumerate(state_refs):
         loads.append(pltpu.make_async_copy(ref, state.at[i], local_sem.at[i]))
@@ -157,7 +162,7 @@
     def h_copy(slot, n):
         first, width = lanes[n]
         spot = hall.at[pl.ds(slot * tokens, tokens), pl.ds(first, width)]
-        source = h_ref.at[:, pl.ds(first, width)]
+        source = h_vm.at[:, pl.ds(first, width)]
         if slot == 3:
             source = hall.at[pl.ds(2 * tokens, tokens), pl.ds(first, width)]
         return remote(
@@ -178,8 +183,8 @@
         return remote(
             ot.at[to_yl, block_at(q), to_c],
             oall.at[q, :, pl.ds(slot * tokens, tokens)],
-            o_send.at[slot - 1, q],
-            o_recv.at[slot - 1, q],
+            o_send.at[slot - 1],
+            o_recv.at[q],
             target,
         )
 
@@ -189,6 +194,7 @@
         oall[q, :, pl.ds(0, tokens)] = ot[yl, block_at(q), c]
         return carry
 
+    h_load.wait()
     h_copy(2, 0).start()
     h_copy(1, 0).start()
 
@@ -207,10 +213,11 @@
         h_copy(2, n).start()
         h_copy(1, n).start()
     lax.fori_loop(1, nz, send_blocks, 0)
-    pair = remote(x_ref, xb.at[pl.ds(yl * roll, roll)], p_send.at[0], p_recv.at[0], across)
+    x_load.wait()
+    pair = remote(x_vm, xb.at[pl.ds(yl * roll, roll)], p_send.at[0], p_recv.at[0], across)
     pair.start()
-    hall[pl.ds(0, tokens), :] = h_ref[...]
-    xb[pl.ds(yl * roll, roll), :] = x_ref[...]
+    hall[pl.ds(0, tokens), :] = h_vm[...]
+    xb[pl.ds(yl * roll, roll), :] = x_vm[...]
 
     def compute(q, slot, way, n):
         first, width = lanes[n]
@@ -219,8 +226,8 @@
         )
 
     def arrived(q):
-        for peer in peers:
-            o_copy(q, *peer).wait_recv()
+        spot = oall.at[q, :, pl.ds(tokens, 3 * tokens)]
+        remote(spot, spot, o_send.at[0], o_recv.at[q], core).wait_recv()
 
     def r_copy(way, sub, n, t):
         first, width = lanes[n]
@@ -228,7 +235,7 @@
         return remote(
             sbuf.at[spot],
             rbuf.at[spot],
-            r_send.at[way, sub, n, t],
+            r_send.at[way, sub],
             r_recv.at[way, sub, n, t],
             ring[way],
         )
@@ -289,19 +296,19 @@
         block = lax.rem(z + nz - t, nz) if way == 0 else lax.rem(z + t, nz)
         spot = wall.at[block, c, pl.ds(sub * half, half), pl.ds(first, width)]
         return remote(
-            spot, spot, w_send.at[way, sub, n, t], w_recv.at[way, sub, n, t], ring[way]
+            spot, spot, w_send.at[way, sub], w_recv.at[way, sub, n, t], ring[way]
         )
 
     def c_copy(way, sub, n, t):
         first, width = lanes[n]
         block = lax.rem(z + 2 * nz - 1 - t, nz) if way == 0 else lax.rem(z + 1 + t, nz)
         spot = wall.at[block, c, pl.ds(sub * half, half), pl.ds(first, width)]
-        return remote(spot, spot, c_send.at[way, sub, n, t], c_recv.at[way, sub, n, t], core)
+        return remote(spot, spot, c_send.at[way, sub], c_recv.at[way, t], core)
 
     def own_copy(sub, n):
         first, width = lanes[n]
         spot = wall.at[z, c, pl.ds(sub * half, half), pl.ds(first, width)]
-        return remote(spot, spot, own_send.at[sub, n], own_recv.at[sub, n], core)
+        return remote(spot, spot, own_send.at[0], own_recv.at[0], core)
 
     for n in pieces:
         for sub in range(2):
@@ -328,8 +335,8 @@
         return remote(
             pbuf.at[j, k],
             xbuf.at[rel - 1, j // 4, k],
-            x_send.at[rel - 1, j // 4, k],
-            x_recv.at[rel - 1, j // 4, k],
+            x_send.at[rel - 1],
+            x_recv.at[j // 4, k],
             {"x": lax.rem(x + rel, 4)},
         )
 
@@ -354,8 +361,8 @@
         return remote(
             ysend.at[to_yl, jj, k],
             ybuf.at[yh, k],
-            y_send.at[to_yl, jj, k],
-            y_recv.at[yh, k],
+            y_send.at[to_yl, jj],
+            y_recv.at[yh],
             {"yl": to_yl, "yh": 2 * yl + jj},
         )
 
@@ -368,8 +375,9 @@
             @pl.when(lax.rem(j, 4) == x)
             def _(j=j, k=k, jj=jj):
                 total = pbuf[j, k].astype(jnp.float32)
+                spot = xbuf.at[:, jj, k]
+                remote(spot, spot, x_send.at[0], x_recv.at[jj, k], core).wait_recv()
                 for rel in range(1, 4):
-                    x_copy(rel, j, k).wait_recv()
                     total += xbuf[rel - 1, jj, k].astype(jnp.float32)
                 for to_yl in range(2):
                     rows = slice(to_yl * roll, (to_yl + 1) * roll)
@@ -408,16 +416,14 @@
 
     def multiply_step(t):
         for way in range(2):
-            for sub in range(2):
-                for n in pieces:
-                    c_copy(way, sub, n, t).wait_recv()
-            multiply(lax.rem(z + nz - 1 - t, nz) if way == 0 else lax.rem(z + 1 + t, nz))
+            block = lax.rem(z + nz - 1 - t, nz) if way == 0 else lax.rem(z + 1 + t, nz)
+            spot = wall.at[block, 1 - c]
+            remote(spot, spot, c_send.at[0, 0], c_recv.at[way, t], core).wait_recv()
+            multiply(block)
 
     pair.wait_recv()
     pass_on(0, steps > 2)
-    for sub in range(2):
-        for n in pieces:
-            own_copy(sub, n).wait_recv()
+    remote(wall.at[0, 0], wall.at[z, 1 - c], own_send.at[0], own_recv.at[0], core).wait_recv()
     multiply(z)
 
     if steps > 3:
@@ -442,9 +448,9 @@
         pass_on(steps - 1, None)
         multiply_step(steps - 2)
         finish(z)
-    for n in pieces:
-        for way in range(2):
-            c_copy(way, way, n, steps - 1).wait_recv()
+    for way in range(2):
+        spot = wall.at[lax.rem(z + steps, nz), 1 - c, pl.ds(way * half, half)]
+        remote(spot, spot, c_send.at[0, 0], c_recv.at[way, steps - 1], core).wait_recv()
     multiply(lax.rem(z + steps, nz))
     finish_step(steps - 2)
     finish(lax.rem(z + steps, nz))
@@ -461,14 +467,9 @@
 
         @pl.when(jnp.logical_not(mine))
         def _(source=source):
-            for k in range(per):
-                remote(
-                    ysend.at[0, 0, 0],
-                    ybuf.at[source, k],
-                    y_send.at[0, 0, 0],
-                    y_recv.at[source, k],
-                    across,
-                ).wait_recv()
+            remote(
+                ysend.at[0, 0], ybuf.at[source], y_send.at[0, 0], y_recv.at[source], across
+            ).wait_recv()
 
         for k in range(per):
             streams[k] += ybuf[source, k].astype(jnp.float32)
@@ -480,12 +481,12 @@
     ss_out[...] = square
 
     def s_copy(r):
-        return remote(ss_out, ss_in.at[r - 1], s_send.at[r - 1], s_recv.at[r - 1], section[r - 1])
+        return remote(ss_out, ss_in.at[r - 1], s_send.at[0], s_recv.at[0], section[r - 1])
 
     for r in range(1, 16):
         s_copy(r).start()
+    remote(ss_in, ss_in, s_send.at[0], s_recv.at[0], core).wait_recv()
     for r in range(1, 16):
-        s_copy(r).wait_recv()
         square += ss_in[r - 1]
     scale = lax.rsqrt(square * (1.0 / (16 * share)) + norm_eps)
     normed = (stream * scale[0:1]).T
@@ -494,55 +495,38 @@
         for i in range(2):
             natural.append(normed[i * roll : (i + 1) * roll, k * half : (k + 1) * half])
     natural = jnp.concatenate(natural, axis=1)
-    out_ref[...] = (natural * gain_ref[...].astype(jnp.float32)).astype(jnp.bfloat16)
+    out_ref[...] = natural
 
     pair.wait_send()
     for slot in range(1, 4):
         for n in pieces:
             h_copy(slot, n).wait_send()
 
-    def drain_blocks(q, carry):
-        for peer in peers:
-            o_copy(q, *peer).wait_send()
-        return carry
-
-    lax.fori_loop(0, nz, drain_blocks, 0)
-    for n in pieces:
-        r_copy(0, 0, n, 0).wait_send()
-        r_copy(1, 1, n, 0).wait_send()
+    def drain(ref, sem):
+        remote(ref, ref, sem, p_recv.at[0], core).wait_send()
+
+    for slot in range(3):
+        drain(ot.at[0, :, 0], o_send.at[slot])
+        drain(xbuf.at[slot], x_send.at[slot])
+    drain(wall.at[0, 0], own_send.at[0])
+    for way in range(2):
         for sub in range(2):
-            own_copy(sub, n).wait_send()
-            w_copy(sub, sub, n, steps - 1).wait_send()
-            c_copy(sub, sub, n, steps - 1).wait_send()
-
-    def drain(t, carry):
-        for way in range(2):
-            for sub in range(2):
-                for n in pieces:
-                    r_copy(way, sub, n, t + 1).wait_send()
-                    w_copy(way, sub, n, t).wait_send()
-                    c_copy(way, sub, n, t).wait_send()
-        return carry
-
-    lax.fori_loop(0, steps - 1, drain, 0)
-    for rel in range(1, 4):
-        for jj in range(2):
-            for k in range(per):
-                x_copy(rel, jj * 4, k).wait_send()
+            count = steps if way == sub else steps - 1
+            for sem in (r_send, w_send, c_send):
+                drain(sbuf.at[way, sub, pl.ds(0, count)], sem.at[way, sub])
     for jj in range(2):
         for to_yl in range(2):
             mine = jnp.logical_and(yl == to_yl, yh == 2 * yl + jj)
 
             @pl.when(jnp.logical_not(mine))
             def _(to_yl=to_yl, jj=jj):
-                for k in range(per):
-                    y_copy(to_yl, jj, k).wait_send()
-
-    for r in range(1, 16):
-        s_copy(r).wait_send()
-
-
-def update_and_decode(nz, hidden_act, out_grad, flat_in, state, resid, gain):
+                spot = ysend.at[to_yl, jj]
+                remote(spot, spot, y_send.at[to_yl, jj], y_recv.at[0], across).wait_send()
+
+    drain(ss_in, s_send.at[0])
+
+
+def update_and_decode(nz, hidden_act, out_grad, flat_in, state, resid):
     tokens, hidden = hidden_act.shape
     cols = state[0].shape[0]
     roll = flat_in.shape[0]
@@ -554,16 +538,17 @@
     vmem = pl.BlockSpec(memory_space=pltpu.VMEM)
     hbm = pl.BlockSpec(memory_space=pl.ANY)
     dma = pltpu.SemaphoreType.DMA
-    links = [dma((2, 2, 2, steps))] * 2
     return pl.pallas_call(
         functools.partial(kernel, nz),
         out_shape=(
             jax.ShapeDtypeStruct((cols, hidden), jnp.float32),
-            jax.ShapeDtypeStruct((roll, share), jnp.bfloat16),
+            jax.ShapeDtypeStruct((roll, share), jnp.float32),
         ),
-        in_specs=[vmem, hbm, vmem, [hbm] * 4, hbm, vmem],
+        in_specs=[hbm, hbm, hbm, [hbm] * 4, hbm],
         out_specs=(vmem, vmem),
         scratch_shapes=[
+            pltpu.VMEM(hidden_act.shape, jnp.bfloat16),
+            pltpu.VMEM(flat_in.shape, jnp.bfloat16),
             pltpu.VMEM(out_grad.shape, jnp.bfloat16),
             pltpu.VMEM((2, nz, 2, cols, tokens), jnp.bfloat16),
             pltpu.VMEM((4 * tokens, hidden), jnp.bfloat16),
@@ -584,22 +569,25 @@
             pltpu.VMEM((span, 2 * roll), jnp.float32),
             dma((3, 2)),
             dma((3, 2)),
-            dma((3, nz)),
-            dma((3, nz)),
-            *links,
-            dma((9,)),
+            dma((3,)),
+            dma((nz,)),
+            dma((2, 2)),
+            dma((2, 2, 2, steps)),
+            dma((11,)),
             dma((1,)),
             dma((1,)),
-            *links,
-            *links,
             dma((2, 2)),
+            dma((2, 2, 2, steps)),
             dma((2, 2)),
-            dma((3, 2, per)),
-            dma((3, 2, per)),
-            dma((2, 2, per)),
-            dma((4, per)),
-            dma((15,)),
-            dma((15,)),
+            dma((2, steps)),
+            dma((1,)),
+            dma((1,)),
+            dma((3,)),
+            dma((2, per)),
+            dma((2, 2)),
+            dma((4,)),
+            dma((1,)),
+            dma((1,)),
         ],
         compiler_params=pltpu.CompilerParams(collective_id=0, has_side_effects=True),
         cost_estimate=pl.CostEstimate(
@@ -608,7 +596,7 @@
             transcendentals=0,
         ),
         name="update_and_decode",
-    )(hidden_act, out_grad, flat_in, list(state), resid, gain)
+    )(hidden_act, out_grad, flat_in, list(state), resid)
 
 
 def per_device(
@@ -628,12 +616,13 @@
     flat_in = decode_in.reshape(flat_rows, hidden_local)
     resid_flat = residual_in.reshape(flat_rows, -1)
     state = (grad_accum.T, master_weight.T, adam_first.T, adam_second.T)
-    grad_share, decoded = update_and_decode(
-        nz, hidden_act, out_grad, flat_in, state, resid_flat, norm_gain[None]
+    grad_share, normed = update_and_decode(
+        nz, hidden_act, out_grad, flat_in, state, resid_flat
     )
     weight_new, first_new, second_new = new_weight(
         grad_share.T + grad_accum, master_weight, adam_first, adam_second
     )
+    decoded = (normed * norm_gain.astype(jnp.float32)).astype(jnp.bfloat16)
     decoded = decoded.reshape(steps_count, roll_rows, -1)
     return (weight_new, first_new, second_new, decoded)
 

time: 102 us -> 98.9 us (0.970)
  Pallas kernels: 96.7 us -> 92.9 us
  other arithmetic: 2.12 us -> 4.31 us
  local copies, waits for them, and re-layouts: 1.88 us -> 0.01 us
    pallas_call x1, Pallas kernels: 96.7 us -> 92.9 us  [update_and_decode(): pl.pallas_call(functools.partial(kernel, nz), out_shape=(jax.ShapeDtypeSt...]
    convert_element_type x0 -> x2, other arithmetic: none -> 2.2 us  [per_device(): decoded = (normed * norm_gain.astype(jnp.float32)).astype(jnp.bfloat16)]
    broadcast_in_dim x1 -> x0, local copies, waits for them, and re-layouts: 1.24 us -> none  [per_device(): norm_gain[None]]
where the time goes in v4:
time: 98.9 us; the launch traced here: 97.8 us
  Pallas kernels  92.9 us (94%)
  other arithmetic  4.31 us (4%)
    pallas_call x1, Pallas kernels, update_and_decode(): pl.pallas_call(functools.partial(kernel, nz), out_shape=(jax.ShapeDtypeSt...  92.9 us
    convert_element_type x2, other arithmetic, per_device(): decoded = (normed * norm_gain.astype(jnp.float32)).astype(jnp.bfloat16)  2.2 us
    sub x1, other arithmetic, new_weight(): master_weight - learn_rate * (update + decay_rate * master_weight)  2.11 us

profile of v4, /device:TPU:6, one launch (start us, length us, event | category | flops | bytes accessed | tf_op | source)
XLA Modules:
  0.0 97.8 jit_solution(9762039587343418981)
XLA Ops:
  0.6 0.7 convert_element_type.6
  1.3 0.0 copy-start
  1.3 0.0 copy-start.1
  1.3 0.0 copy-start.2
  1.3 0.0 copy-start.3
  1.3 92.9 %update_and_decode.1 = (f32[96,896]{1,0:T(8,128)}, f32[64,288]{1,0:T(8,128)}) custom-call(bf16[128,896]{1,0:T(8,128)(2,1)} %h_ref.1, bf16[128,4608]{1,0:T(8,128)(2,1)} %o_ref.1, bf16[64,896]{1,0:T(8,128)(2,1)} %bitcast.21, f32[96,896]{1,0:T(8,128)} %bitcast.16, f32[96,896]{1,0:T(8,128)} %bitcast.15, f32[96,896]{1,0:T(8,128)} %bitcast.17, ...), custom_call_target="tpu_custom_call" | custom-call | flops 1585446912 | bytes 3000000 | tf_op jit(solution)/shard_map/update_and_decode/pallas_call | solution.py:541
  94.2 1.5 %multiply_convert_fusion = bf16[64,288]{1,0:T(8,128)(2,1)} fusion(f32[64,288]{1,0:T(8,128)} %get-tuple-element.7, f32[288]{0:T(512)S(1)} %convert_element_type.6), kind=kLoop, calls=%fused_computation.5 | loop fusion | flops 36864 | bytes 111744 | tf_op jit(solution)/shard_map/convert_element_type | solution.py:625
  95.7 0.0 copy-done
  95.7 0.0 copy-done.1
  95.7 0.0 copy-done.2
  95.7 0.0 copy-done.3
  95.7 2.1 %multiply_subtract_fusion = (f32[896,96]{0,1:T(8,128)}, f32[896,96]{0,1:T(8,128)}, f32[896,96]{0,1:T(8,128)}) fusion(f32[896,96]{0,1:T(8,128)S(1)} %copy-done, f32[896,96]{0,1:T(8,128)S(1)} %copy-done.1, f32[96,896]{1,0:T(8,128)} %get-tuple-element.6, f32[896,96]{0,1:T(8,128)S(1)} %copy-done.2, f32[896,96]{0,1:T(8,128)S(1)} %copy-done.3), kind=kLoop, calls=%fused_computation.3 | loop fusion | flops 1376256 | bytes 2752512 | tf_op jit(solution)/shard_map/sub | solution.py:54
Async XLA Ops:
  1.3 94.4 %copy-start = (f32[896,96]{0,1:T(8,128)S(1)}, f32[896,96]{0,1:T(8,128)}, u32[]{:S(2)}) copy-start(f32[896,96]{0,1:T(8,128)} %param.12) | copy-start | bytes 1032196
  1.3 94.4 %copy-start.1 = (f32[896,96]{0,1:T(8,128)S(1)}, f32[896,96]{0,1:T(8,128)}, u32[]{:S(2)}) copy-start(f32[896,96]{0,1:T(8,128)} %param.11) | copy-start | bytes 1032196
  1.3 94.4 %copy-start.2 = (f32[896,96]{0,1:T(8,128)S(1)}, f32[896,96]{0,1:T(8,128)}, u32[]{:S(2)}) copy-start(f32[896,96]{0,1:T(8,128)} %param.13) | copy-start | bytes 1032196
  1.3 94.4 %copy-start.3 = (f32[896,96]{0,1:T(8,128)S(1)}, f32[896,96]{0,1:T(8,128)}, u32[]{:S(2)}) copy-start(f32[896,96]{0,1:T(8,128)} %param.14) | copy-start | bytes 1032196

commit v5 on v4

--- a/solution.py
+++ b/solution.py
@@ -249,7 +249,7 @@
         sbuf[way, sub, t, :, pl.ds(first, width)] = value.astype(jnp.bfloat16)
         r_copy(way, sub, n, t).start()
 
-    for n in pieces:
+    def first_push(n):
         h_copy(2, n).wait_recv()
         h_copy(3, n).start()
         h_copy(1, n).wait_recv()
@@ -260,36 +260,50 @@
         push(0, 0, n, 0, 0, 0, False)
         push(1, 1, n, 0, 0, 0, False)
 
-    def fill(t):
+    def fill(t, n):
         slot = lax.rem(t, 2)
         for way in range(2):
-            arrived(2 * t - 1 + way)
-            for n in pieces:
-                compute(2 * t - 1 + way, slot, way, n)
-
-    fill(1)
-    for n in pieces:
+            if n == 0:
+                arrived(2 * t - 1 + way)
+            compute(2 * t - 1 + way, slot, way, n)
+
+    def push_all(n, t, receive=True):
+        slot = lax.rem(t, 2)
         for sub in range(2):
-            push(0, sub, n, 1, 1, 0, sub == 0)
-            push(1, 1 - sub, n, 1, 1, 1, sub == 0)
+            push(0, sub, n, t, slot, 0, receive or sub == 0)
+            push(1, 1 - sub, n, t, slot, 1, receive or sub == 0)
+
+    first_push(0)
+    fill(1, 0)
+    for n in pieces[1:]:
+        first_push(n)
+    push_all(0, 1, False)
+    for n in pieces[1:]:
+        fill(1, n)
+    fill(2, 0)
+    push_all(0, 2)
+    for n in pieces[1:]:
+        push_all(n, 1, False)
 
     def step(t, carry):
-        fill(t)
-        slot = lax.rem(t, 2)
-        for n in pieces:
-            for sub in range(2):
-                push(0, sub, n, t, slot, 0, True)
-                push(1, 1 - sub, n, t, slot, 1, True)
+        fill(t, 0)
+        for n in pieces[1:]:
+            fill(t - 1, n)
+        push_all(0, t)
+        for n in pieces[1:]:
+            push_all(n, t - 1)
         return carry
 
-    lax.fori_loop(2, steps, step, 0)
+    lax.fori_loop(3, steps, step, 0)
+    for n in pieces[1:]:
+        fill(steps - 1, n)
 
     for load in loads:
         load.wait()
     turned[...] = window[...].astype(jnp.float32).T
     arrived(nz - 1)
     for n in pieces:
-        compute(nz - 1, 0, 0, n)
+        compute(nz - 1, steps % 2, 0, n)
 
     def w_copy(way, sub, n, t):
         first, width = lanes[n]
@@ -310,11 +324,11 @@
         spot = wall.at[z, c, pl.ds(sub * half, half), pl.ds(first, width)]
         return remote(spot, spot, own_send.at[0], own_recv.at[0], core)
 
-    for n in pieces:
+    def settle(n):
         for sub in range(2):
             first, width = lanes[n]
             here = (pl.ds(sub * half, half), pl.ds(first, width))
-            value = part[0, 0, here[0], here[1]]
+            value = part[steps % 2, 0, here[0], here[1]]
             for way in range(2):
                 r_copy(way, sub, n, steps - 1).wait_recv()
                 value += rbuf[way, sub, steps - 1, :, here[1]].astype(jnp.float32)
@@ -399,20 +413,15 @@
         finish(lax.rem(z + nz - 1 - t, nz))
         finish(lax.rem(z + 1 + t, nz))
 
-    def pass_on(t, short):
-        for n in pieces:
-            for sub in range(2):
-                for way in range(2):
-                    if way == sub:
-                        w_copy(way, sub, n, t).wait_recv()
-                        if short is not None:
-                            w_copy(way, sub, n, t + 1).start()
-                        c_copy(way, sub, n, t).start()
-                    elif short is not None:
-                        w_copy(way, sub, n, t).wait_recv()
-                        if short:
-                            w_copy(way, sub, n, t + 1).start()
-                        c_copy(way, sub, n, t).start()
+    def pass_on(n, t):
+        for sub in range(2):
+            for way in range(2):
+                last = steps - 1 if way == sub else steps - 2
+                if t <= last:
+                    w_copy(way, sub, n, t).wait_recv()
+                    if t < last:
+                        w_copy(way, sub, n, t + 1).start()
+                    c_copy(way, sub, n, t).start()
 
     def multiply_step(t):
         for way in range(2):
@@ -421,33 +430,29 @@
             remote(spot, spot, c_send.at[0, 0], c_recv.at[way, t], core).wait_recv()
             multiply(block)
 
+    settle(0)
+    for n in pieces[1:]:
+        push_all(n, steps - 1)
+    pass_on(0, 0)
+    for n in pieces[1:]:
+        settle(n)
     pair.wait_recv()
-    pass_on(0, steps > 2)
-    remote(wall.at[0, 0], wall.at[z, 1 - c], own_send.at[0], own_recv.at[0], core).wait_recv()
-    multiply(z)
-
-    if steps > 3:
-        pass_on(1, True)
-        multiply_step(0)
-        finish(z)
-
-        def w_step(t, carry):
-            pass_on(t, True)
+    for t in range(steps):
+        if t < steps - 1:
+            pass_on(0, t + 1)
+        for n in pieces[1:]:
+            pass_on(n, t)
+        if t == 0:
+            remote(
+                wall.at[0, 0], wall.at[z, 1 - c], own_send.at[0], own_recv.at[0], core
+            ).wait_recv()
+            multiply(z)
+        else:
             multiply_step(t - 1)
+        if t == 1:
+            finish(z)
+        if t > 1:
             finish_step(t - 2)
-            return carry
-
-        lax.fori_loop(2, steps - 2, w_step, 0)
-        pass_on(steps - 2, False)
-        multiply_step(steps - 3)
-        finish_step(steps - 4)
-        pass_on(steps - 1, None)
-        multiply_step(steps - 2)
-        finish_step(steps - 3)
-    else:
-        pass_on(steps - 1, None)
-        multiply_step(steps - 2)
-        finish(z)
     for way in range(2):
         spot = wall.at[lax.rem(z + steps, nz), 1 - c, pl.ds(way * half, half)]
         remote(spot, spot, c_send.at[0, 0], c_recv.at[way, steps - 1], core).wait_recv()

time: 98.9 us -> 103 us (1.041); the launches traced: 97.8 us -> 103 us
  Pallas kernels: 92.9 us -> 98.1 us
    pallas_call x1, Pallas kernels: 92.9 us -> 98.1 us  [update_and_decode(): pl.pallas_call(functools.partial(kernel, nz), out_shape=(jax.ShapeDtypeSt...]
where the time goes in v5:
time: 103 us
  Pallas kernels  98.1 us (95%)
  other arithmetic  4.31 us (4%)
    pallas_call x1, Pallas kernels, update_and_decode(): pl.pallas_call(functools.partial(kernel, nz), out_shape=(jax.ShapeDtypeSt...  98.1 us
    convert_element_type x2, other arithmetic, per_device(): decoded = (normed * norm_gain.astype(jnp.float32)).astype(jnp.bfloat16)  2.2 us
    sub x1, other arithmetic, new_weight(): master_weight - learn_rate * (update + decay_rate * master_weight)  2.11 us

profile of v5, /device:TPU:6, one launch (start us, length us, event | category | flops | bytes accessed | tf_op | source)
XLA Modules:
  0.0 103.0 jit_solution(3688037825574268417)
XLA Ops:
  0.6 0.7 convert_element_type.6
  1.3 0.0 copy-start
  1.3 0.0 copy-start.1
  1.3 0.0 copy-start.2
  1.3 0.0 copy-start.3
  1.3 98.1 %update_and_decode.1 = (f32[96,896]{1,0:T(8,128)}, f32[64,288]{1,0:T(8,128)}) custom-call(bf16[128,896]{1,0:T(8,128)(2,1)} %h_ref.1, bf16[128,4608]{1,0:T(8,128)(2,1)} %o_ref.1, bf16[64,896]{1,0:T(8,128)(2,1)} %bitcast.21, f32[96,896]{1,0:T(8,128)} %bitcast.16, f32[96,896]{1,0:T(8,128)} %bitcast.15, f32[96,896]{1,0:T(8,128)} %bitcast.17, ...), custom_call_target="tpu_custom_call" | custom-call | flops 1585446912 | bytes 3000000 | tf_op jit(solution)/shard_map/update_and_decode/pallas_call | solution.py:546
  99.4 1.5 %multiply_convert_fusion = bf16[64,288]{1,0:T(8,128)(2,1)} fusion(f32[64,288]{1,0:T(8,128)} %get-tuple-element.7, f32[288]{0:T(512)S(1)} %convert_element_type.6), kind=kLoop, calls=%fused_computation.5 | loop fusion | flops 36864 | bytes 111744 | tf_op jit(solution)/shard_map/convert_element_type | solution.py:630
  100.9 0.0 copy-done
  100.9 0.0 copy-done.1
  100.9 0.0 copy-done.2
  100.9 0.0 copy-done.3
  100.9 2.1 %multiply_subtract_fusion = (f32[896,96]{0,1:T(8,128)}, f32[896,96]{0,1:T(8,128)}, f32[896,96]{0,1:T(8,128)}) fusion(f32[896,96]{0,1:T(8,128)S(1)} %copy-done, f32[896,96]{0,1:T(8,128)S(1)} %copy-done.1, f32[96,896]{1,0:T(8,128)} %get-tuple-element.6, f32[896,96]{0,1:T(8,128)S(1)} %copy-done.2, f32[896,96]{0,1:T(8,128)S(1)} %copy-done.3), kind=kLoop, calls=%fused_computation.3 | loop fusion | flops 1376256 | bytes 2752512 | tf_op jit(solution)/shard_map/sub | solution.py:54
Async XLA Ops:
  1.3 99.6 %copy-start = (f32[896,96]{0,1:T(8,128)S(1)}, f32[896,96]{0,1:T(8,128)}, u32[]{:S(2)}) copy-start(f32[896,96]{0,1:T(8,128)} %param.12) | copy-start | bytes 1032196
  1.3 99.6 %copy-start.1 = (f32[896,96]{0,1:T(8,128)S(1)}, f32[896,96]{0,1:T(8,128)}, u32[]{:S(2)}) copy-start(f32[896,96]{0,1:T(8,128)} %param.11) | copy-start | bytes 1032196
  1.3 99.6 %copy-start.2 = (f32[896,96]{0,1:T(8,128)S(1)}, f32[896,96]{0,1:T(8,128)}, u32[]{:S(2)}) copy-start(f32[896,96]{0,1:T(8,128)} %param.13) | copy-start | bytes 1032196
  1.3 99.6 %copy-start.3 = (f32[896,96]{0,1:T(8,128)S(1)}, f32[896,96]{0,1:T(8,128)}, u32[]{:S(2)}) copy-start(f32[896,96]{0,1:T(8,128)} %param.14) | copy-start | bytes 1032196
